TPU v7x, 256 devices: a whole 4x4x8 slice. The times are simulated.
256 devices in a mesh: ens: 16 (over z_lo, y), space: 16 (over z_hi, x, core).
Axes of the slice: x: 4, y: 4, z: 8 (z_hi: 2, z_lo: 4; z = z_hi * 4 + z_lo), core: 2. Of those that a mesh axis runs over, the one named last changes fastest.
Arguments:
- grid_hidden: bfloat16 [16, 2048, 1024], P('ens', 'space'), may hold values from -600 to 600
- latent: bfloat16 [16, 2048, 1024], P('ens', 'space'), may hold values from -6 to 6
- tile_neighbor_index: int32 [16, 128], P('space'), may hold values from 0 to 2047, as said below
- target: float32 [100, 2048], P(None, 'space'), may hold values from -6 to 6
- w_query: bfloat16 [1024, 1024], replicated, may hold values from -0.1875 to 0.1875
- w_key: bfloat16 [1024, 1024], replicated, may hold values from -0.1875 to 0.1875
- w_value: bfloat16 [1024, 1024], replicated, may hold values from -0.1875 to 0.1875
- w_mix: bfloat16 [1024, 1024], replicated, may hold values from -0.1875 to 0.1875
- readout_weight: bfloat16 [100, 1024], replicated, may hold values from -0.1875 to 0.1875
Outputs:
- fair_ranked_score_loss: float32 [], replicated
- grad_out: float32 [100, 1024], replicated
- grad_query: float32 [1024, 1024], P('ens', 'space')
- grad_key: float32 [1024, 1024], P('ens', 'space')
- grad_value: float32 [1024, 1024], P('ens', 'space')
- grad_mix: float32 [1024, 1024], P('ens', 'space')
Inputs may be any that keep to these rules, and one draw needn't show every extreme that they name: `tile_neighbor_index`: row t holds 128 distinct latent node indices, all among the nodes of space shard s = t and of the two shards beside it, counted cyclically; shard s holds nodes s * 128 to (s + 1) * 128 - 1.
All inputs are finite; a program needn't handle non-finite values.
Results may differ from a plain program's by a relative error of at most 0.025.
Values may be sent and summed in bfloat16 or wider, within the bound.
A program may use at most 128 MiB of HBM per device.

v0:
```python
import jax
import jax.numpy as jnp
from jax import lax
from jax.sharding import PartitionSpec as P

HEADS = 16


EPS = 1e-06
SMOOTH = 0.01


def with_halo(value, sides, width):
    for axis, dim in sides:
        size, length = (lax.axis_size(axis), value.shape[dim])
        up = [(i, (i + 1) % size) for i in range(size)]
        down = [(j, i) for i, j in up]
        last = lax.slice_in_dim(value, length - width, length, axis=dim)
        leading = lax.slice_in_dim(value, 0, width, axis=dim)
        before = lax.ppermute(last, axis, up)
        after = lax.ppermute(leading, axis, down)
        value = jnp.concatenate([before, value, after], axis=dim)
    return value


def packed_total(arrays, axis):
    line, at, done = (jnp.concatenate([a.reshape(-1) for a in arrays]), 0, [])
    subtotal = lax.psum(line, axis)
    for a in arrays:
        done.append(subtotal[at : at + a.size].reshape(a.shape))
        at += a.size
    return tuple(done)


def sent_together(arrays, axis, dim, along):
    ends, at = ([], 0)
    for a in arrays[:-1]:
        at += a.shape[along]
        ends.append(at)
    both = jnp.concatenate(arrays, axis=along)
    return tuple(
        jnp.split(lax.psum_scatter(both, axis, scatter_dimension=dim, tiled=True), ends, axis=along)
    )


def by_heads(values_in):
    return values_in.reshape(
        values_in.shape[0], values_in.shape[1], HEADS, values_in.shape[2] // HEADS
    )


def rows_times(blocks, matrix):
    flat_rows = blocks.reshape(-1, blocks.shape[-1])
    product = jnp.dot(flat_rows, matrix, preferred_element_type=jnp.float32)
    return product.reshape(blocks.shape[:-1] + (matrix.shape[1],))


def contract_rows(left_side, right_side):
    return lax.dot_general(
        left_side, right_side, (((0,), (0,)), ((), ())), preferred_element_type=jnp.float32
    )


def contracted_columns(left_side, right_side):
    return lax.dot_general(
        left_side, right_side, (((1,), (1,)), ((), ())), preferred_element_type=jnp.float32
    )


def decoder_forward(grid_point_rows, latent_node_rows, weight_params):
    w_query, w_key, w_value, w_mix, readout_weight = weight_params
    features = grid_point_rows.shape[-1]
    factor = (features // HEADS) ** (-0.5)
    queries = rows_times(grid_point_rows, w_query).astype(jnp.bfloat16)
    keyset = rows_times(latent_node_rows, w_key).astype(jnp.bfloat16)
    valueset = rows_times(latent_node_rows, w_value).astype(jnp.bfloat16)
    scores = (
        jnp.einsum(
            "tqhd,tkhd->thqk",
            by_heads(queries),
            by_heads(keyset),
            preferred_element_type=jnp.float32,
        )
        * factor
    )
    highest = jnp.max(scores, axis=-1, keepdims=True)
    raised = jnp.exp(scores - highest)
    softmaxed = raised / jnp.sum(raised, axis=-1, keepdims=True)
    softmaxed_b = softmaxed.astype(jnp.bfloat16)
    attended = jnp.einsum(
        "thqk,tkhd->tqhd", softmaxed_b, by_heads(valueset), preferred_element_type=jnp.float32
    )
    attended = attended.reshape(grid_point_rows.shape).astype(jnp.bfloat16)
    hidden = grid_point_rows.astype(jnp.float32) + rows_times(attended, w_mix)
    inverse = lax.rsqrt(jnp.mean(hidden * hidden, axis=-1, keepdims=True) + EPS)
    normed = hidden * inverse
    normed_backward = normed.astype(jnp.bfloat16).reshape(-1, features)
    member_prediction = contracted_columns(readout_weight, normed_backward)
    saved_activations = (
        grid_point_rows,
        latent_node_rows,
        queries,
        keyset,
        valueset,
        softmaxed,
        softmaxed_b,
        attended,
        inverse,
        normed,
        normed_backward,
    )
    return (member_prediction, saved_activations)


def backward(saved_activations, loss_slopes, weight_params):
    w_query, w_key, w_value, w_mix, readout_weight = weight_params
    (
        grid_point_rows,
        latent_node_rows,
        queries,
        keyset,
        valueset,
        softmaxed,
        softmaxed_b,
        attended,
        inverse,
        normed,
        normed_backward,
    ) = saved_activations
    features = grid_point_rows.shape[-1]
    factor = (features // HEADS) ** (-0.5)
    slopes_b = loss_slopes.astype(jnp.bfloat16)
    grad_out = jnp.dot(slopes_b, normed_backward, preferred_element_type=jnp.float32)
    d_normed = contract_rows(slopes_b, readout_weight)
    normed_rows = normed.reshape(-1, features)
    d_hidden = inverse.reshape(-1, 1) * (
        d_normed - normed_rows * jnp.mean(d_normed * normed_rows, axis=-1, keepdims=True)
    )
    d_hidden_b = d_hidden.astype(jnp.bfloat16)
    grad_mix = contract_rows(attended.reshape(-1, features), d_hidden_b)
    d_attended = (
        contracted_columns(d_hidden_b, w_mix).astype(jnp.bfloat16).reshape(grid_point_rows.shape)
    )
    d_probs = jnp.einsum(
        "tqhd,tkhd->thqk",
        by_heads(d_attended),
        by_heads(valueset),
        preferred_element_type=jnp.float32,
    )
    d_values = jnp.einsum(
        "thqk,tqhd->tkhd", softmaxed_b, by_heads(d_attended), preferred_element_type=jnp.float32
    )
    d_values = d_values.reshape(latent_node_rows.shape).astype(jnp.bfloat16)
    d_scores = softmaxed * (d_probs - jnp.sum(d_probs * softmaxed, axis=-1, keepdims=True)) * factor
    d_scores_b = d_scores.astype(jnp.bfloat16)
    d_queries = jnp.einsum(
        "thqk,tkhd->tqhd", d_scores_b, by_heads(keyset), preferred_element_type=jnp.float32
    )
    d_queries = d_queries.reshape(grid_point_rows.shape).astype(jnp.bfloat16)
    d_keys = jnp.einsum(
        "thqk,tqhd->tkhd", d_scores_b, by_heads(queries), preferred_element_type=jnp.float32
    )
    d_keys = d_keys.reshape(latent_node_rows.shape).astype(jnp.bfloat16)
    grid_flat = grid_point_rows.reshape(-1, features)
    node_flat = latent_node_rows.reshape(-1, features)
    grad_query = contract_rows(grid_flat, d_queries.reshape(-1, features))
    grad_key = contract_rows(node_flat, d_keys.reshape(-1, features))
    grad_value = contract_rows(node_flat, d_values.reshape(-1, features))
    return (grad_out, grad_query, grad_key, grad_value, grad_mix)


def member_ranked_score(member_own_field, members_all, truth_rows, loss_scale_weight):
    members_count = members_all.shape[0]
    to_truth = member_own_field - truth_rows[None]
    skill_term = jnp.sqrt(to_truth * to_truth + SMOOTH)

    def add_member(running, other_member):
        apart_by = member_own_field - other_member[None]
        spread = jnp.sqrt(apart_by * apart_by + SMOOTH)
        return ((running[0] + spread, running[1] + apart_by / spread), None)

    zero_field = jnp.zeros(member_own_field.shape, jnp.float32)
    (spread_sum, slope_sum), _ = lax.scan(add_member, (zero_field, zero_field), members_all)
    pair_weight = 1.0 / (members_count * (members_count - 1))
    loss_part = loss_scale_weight * (
        jnp.sum(skill_term) / members_count
        - 0.5 * pair_weight * jnp.sum(spread_sum - jnp.sqrt(jnp.float32(SMOOTH)))
    )
    loss_slopes = loss_scale_weight * (
        to_truth / skill_term / members_count - pair_weight * slope_sum
    )
    return (loss_part, loss_slopes)


def body(
    grid_hidden, latent, tile_neighbor_index, target, w_query, w_key, w_value, w_mix, readout_weight
):
    node_count = latent.shape[1]
    features = latent.shape[2]
    shards = lax.axis_size("space")
    shard_index = lax.axis_index("space")
    weight_params = (w_query, w_key, w_value, w_mix, readout_weight)
    rimmed = with_halo(latent, (("space", 1),), node_count)
    positions = jnp.mod(tile_neighbor_index - (shard_index - 1) * node_count, node_count * shards)
    latent_node_rows = jnp.take(rimmed[0], positions, axis=0)
    grid_point_rows = grid_hidden[0].reshape(-1, 128, features)
    member_prediction, saved_activations = decoder_forward(
        grid_point_rows, latent_node_rows, weight_params
    )
    member_own_field = member_prediction[None]
    loss_scale_weight = (target.shape[0] * target.shape[1] * shards) ** (-0.5)
    members_count = lax.axis_size("ens")
    slice_width = target.shape[1] // members_count
    spread_out = lax.all_to_all(member_own_field, "ens", split_axis=2, concat_axis=0, tiled=True)
    truth_rows = lax.dynamic_slice_in_dim(
        target, lax.axis_index("ens") * slice_width, slice_width, 1
    )
    loss_part, member_slopes = member_ranked_score(
        spread_out, spread_out, truth_rows, loss_scale_weight
    )
    loss_slopes = lax.all_to_all(
        member_slopes.astype(jnp.bfloat16), "ens", split_axis=0, concat_axis=2, tiled=True
    ).astype(member_slopes.dtype)
    grad_out, grad_query, grad_key, grad_value, grad_mix = backward(
        saved_activations, loss_slopes[0], weight_params
    )
    fair_ranked_score_loss, grad_out = packed_total((loss_part, grad_out), ("ens", "space"))
    gradients = (grad_query, grad_key, grad_value, grad_mix)
    gradients = tuple(
        (
            part.astype(jnp.float32)
            for part in sent_together(
                (
                    gradients[0].astype(jnp.bfloat16),
                    gradients[1].astype(jnp.bfloat16),
                    gradients[2].astype(jnp.bfloat16),
                    gradients[3].astype(jnp.bfloat16),
                ),
                "ens",
                0,
                1,
            )
        )
    )
    gradients = tuple(
        (
            part.astype(jnp.float32)
            for part in sent_together(
                (
                    gradients[0].astype(jnp.bfloat16),
                    gradients[1].astype(jnp.bfloat16),
                    gradients[2].astype(jnp.bfloat16),
                    gradients[3].astype(jnp.bfloat16),
                ),
                "space",
                1,
                0,
            )
        )
    )
    return (
        fair_ranked_score_loss,
        grad_out,
        gradients[0],
        gradients[1],
        gradients[2],
        gradients[3],
    )


def solution(mesh):
    in_specs = (
        P("ens", "space", None),
        P("ens", "space", None),
        P("space", None),
        P(None, "space"),
        P(),
        P(),
        P(),
        P(),
        P(),
    )
    out_specs = (
        P(),
        P(),
        P("ens", "space"),
        P("ens", "space"),
        P("ens", "space"),
        P("ens", "space"),
    )
    return jax.shard_map(body, mesh=mesh, in_specs=in_specs, out_specs=out_specs, check_vma=False)
```

profile of v0, /device:TPU:6, one launch (start us, length us, event | category | flops | bytes accessed | tf_op | source)
XLA Modules:
  0.0 400.4 jit_solution(13145849180003600466)
XLA Ops:
  8.1 1.7 collective-permute-start.1
  9.9 2.1 convolution_convert_fusion.9
  12.0 0.8 copy.48
  12.9 1.2 collective-permute-done
  14.1 2.6 collective-permute-done.1
  16.7 1.0 maximum_bitcast_fusion
  17.7 0.9 gather_fusion
  18.6 2.1 convolution_convert_fusion.8
  20.9 2.2 convolution_convert_fusion.10
  23.2 1.5 fusion.45
  24.7 1.7 convolution_convert_fusion.7
  26.5 0.5 multiply_reduce_fusion.1
  27.1 0.4 copy-done.4
  27.5 0.9 convolution_bitcast_fusion.1
  28.4 1.5 copy.51
  29.9 6.0 %all-to-all-start = ((f32[1,100,128]{1,0,2:T(1,128)}), f32[1,100,128]{1,0,2:T(1,128)S(1)}, u32[]{:S(2)}, u32[]{:S(2)}) async-start(f32[1,100,128]{1,0,2:T(1,128)} %copy.51), calls=%async_computation | async-start | bytes 131072 | tf_op jit(solution)/shard_map/all_to_all | solution.py:214
  36.0 0.9 constant_dynamic-slice_fusion
  37.0 7.4 %all-to-all-done = f32[1,100,128]{1,0,2:T(1,128)S(1)} async-done(((f32[1,100,128]{1,0,2:T(1,128)}), f32[1,100,128]{1,0,2:T(1,128)S(1)}, u32[]{:S(2)}, u32[]{:S(2)}) %all-to-all-start) | async-done | bytes 51232 | tf_op jit(solution)/shard_map/all_to_all | solution.py:214
  44.4 1.5 while.13
  45.8 0.6 fusion.26
  46.5 10.7 %all_to_all.33 = bf16[16,100,8]{1,2,0:T(8,128)(2,1)S(1)} all-to-all(bf16[16,100,8]{1,2,0:T(8,128)(2,1)S(1)} %get-tuple-element.81), channel_id=1, replica_groups=mesh['ens'=16,'space'=16] {'ens'}, dimensions={0} | all-to-all | bytes 51200 | tf_op jit(solution)/shard_map/all_to_all | solution.py:221
  57.2 1.2 fusion.13
  58.6 1.5 convolution_convert_fusion.6
  60.1 1.8 copy.53
  61.9 2.6 convolution_convert_fusion.3
  64.5 2.4 fusion.46
  66.9 3.5 convolution_convert_fusion.5
  70.4 3.5 convolution_convert_fusion.4
  73.9 1.8 convolution_convert_fusion.2
  75.7 0.7 convert_bitcast_fusion
  76.4 0.8 convolution_convert_fusion.1
  77.2 0.8 convolution_convert_fusion
  78.0 4.0 pad_maximum_fusion
  82.0 11.3 %copy.65 = bf16[1024,4096]{1,0:T(8,128)(2,1)} copy(bf16[1024,4096]{0,1:T(8,128)(2,1)} %pad_maximum_fusion) | data formatting | bytes 16777216
  93.3 0.6 add_reduce_fusion
  95.6 0.9 pad_maximum_fusion.2
  96.6 109.0 %reduce-scatter.7.cloned.1.call-done = bf16[64,4096]{1,0:T(8,128)(2,1)} async-done(((bf16[1024,4096]{1,0:T(8,128)(2,1)}), bf16[64,4096]{1,0:T(8,128)(2,1)}) %reduce-scatter.7.cloned.1.call-update) | async-done | bytes 524304
  205.6 1.1 fusion.44
  207.5 1.1 pad_maximum_fusion.1
  208.6 177.5 %all-reduce.2.cloned.1.call-done = f32[102401]{0:T(1024)} async-done(((f32[102401]{0:T(1024)}), f32[102401]{0:T(1024)}) %all-reduce.2.cloned.1.call-update) | async-done | bytes 409620 | tf_op jit(solution)/shard_map/psum | solution.py:28
  386.1 1.2 slice.11
  387.3 0.8 reshape.251
  388.1 1.2 slice.10
  389.3 0.9 slice_convert_fusion
  390.2 0.7 copy.60
  390.9 0.7 copy.59
  391.6 0.7 copy.58
  392.3 0.7 copy.57
  (79 shorter events, 2.9 us)
Async XLA Ops:
  8.0 18.5 %copy-start = (bf16[1024,1024]{1,0:T(8,128)(2,1)S(1)}, bf16[1024,1024]{1,0:T(8,128)(2,1)}, u32[]{:S(2)}) copy-start(bf16[1024,1024]{1,0:T(8,128)(2,1)} %param.18) | copy-start | bytes 6291460
  8.0 8.7 %copy-start.8 = (bf16[1,128,1024]{2,1,0:T(8,128)(2,1)S(1)}, bf16[1,128,1024]{2,1,0:T(8,128)(2,1)}, u32[]{:S(2)}) copy-start(bf16[1,128,1024]{2,1,0:T(8,128)(2,1)} %param.12) | copy-start | bytes 786436
  8.0 4.8 %copy-start.11 = (s32[1,128]{1,0:T(1,128)S(1)}, s32[1,128]{1,0:T(1,128)}, u32[]{:S(2)}) copy-start(s32[1,128]{1,0:T(1,128)} %param.13) | copy-start | bytes 1540
  8.0 6.1 %collective-permute-start = (bf16[1,128,1024]{2,1,0:T(8,128)(2,1)}, bf16[1,128,1024]{2,1,0:T(8,128)(2,1)S(1)}, u32[]{:S(2)}, u32[]{:S(2)}) collective-permute-start(bf16[1,128,1024]{2,1,0:T(8,128)(2,1)} %param.12), channel_id=1, source_target_pairs={{0,1},{1,2},{2,3},{3,4},{4,5},{5,6},{6,7},{7,8},{8,9},{9,10},{10,1... | collective-permute-start | bytes 786440 | tf_op jit(solution)/shard_map/ppermute | solution.py:20
  8.1 8.6 %collective-permute-start.1 = (bf16[1,128,1024]{2,1,0:T(8,128)(2,1)}, bf16[1,128,1024]{2,1,0:T(8,128)(2,1)}, u32[]{:S(2)}, u32[]{:S(2)}) collective-permute-start(bf16[1,128,1024]{2,1,0:T(8,128)(2,1)} %param.12), channel_id=1, source_target_pairs={{1,0},{2,1},{3,2},{4,3},{5,4},{6,5},{7,6},{8,7},{9,8},{10,9},{11,1... | collective-permute-start | bytes 786440 | tf_op jit(solution)/shard_map/ppermute | solution.py:21
  20.7 2.6 copy-start.6
  20.9 3.9 copy-start.7
  23.2 3.2 copy-start.2
  24.7 1.7 copy-start.1
  26.5 3.5 copy-start.3
  26.5 1.0 copy-start.4
  29.9 14.4 %all-to-all-start = ((f32[1,100,128]{1,0,2:T(1,128)}), f32[1,100,128]{1,0,2:T(1,128)S(1)}, u32[]{:S(2)}, u32[]{:S(2)}) async-start(f32[1,100,128]{1,0,2:T(1,128)} %copy.51), calls=%async_computation | async-start | bytes 131072 | tf_op jit(solution)/shard_map/all_to_all | solution.py:214
  36.0 169.6 %reduce-scatter.7.cloned.1.call-start = ((), (), s32[]{:S(2)}) async-start(), calls=%async_computation.6 | async-start | bytes 8912896
  73.9 1.8 copy-start.5
  73.9 2.5 copy-start.10
  75.7 1.5 copy-start.9
  93.3 292.8 %all-reduce.2.cloned.1.call-start = ((), (), s32[]{:S(2)}) async-start(), calls=%async_computation.4 | async-start | bytes 827392 | tf_op jit(solution)/shard_map/psum | solution.py:28
  96.5 292.7 %reduce-scatter.5.cloned.1.call-start = ((), (), s32[]{:S(2)}) async-start(), calls=%async_computation.5 | async-start | bytes 557056 | tf_op jit(solution)/shard_map/reduce_scatter | solution.py:42
Sparse Core Ops, SparseCore 0:
  93.4 112.1 reduce-scatter.6
  209.6 74.1 reduce-scatter.4
Sparse Core Ops, SparseCore 1:
  99.8 286.2 all-reduce.1
where the time goes:
time: 402 us; the launch traced here: 400 us
  waiting for transfers between devices  298 us (74%)
  matrix products  30 us (7%)
  local copies, waits for them, and re-layouts  26.1 us (6%)
  between operations  17.1 us (4%)
  blocking collectives  10.7 us (3%)
  other arithmetic  10.3 us (3%)
  starting transfers between devices  7.98 us (2%)
    psum x1, waiting for transfers between devices, packed_total(): subtotal = lax.psum(line, axis)  177 us
    unnamed x4, waiting for transfers between devices  109 us
    unnamed x33, local copies, waits for them, and re-layouts  15.2 us
    all_to_all x1, blocking collectives, body(): lax.all_to_all(member_slopes.astype(jnp.bfloat16), 'ens', split_axis=0, c...  10.7 us
  transfers between devices with their start and end apart: 6, of which 5 were waited for; matrix products, arithmetic and copies ran while one was open for 3% of the time, Pallas kernels for 0%

commit v1 on v0

v1 whole, which is shorter than its diff:
```python
import functools

import jax
import jax.numpy as jnp
from jax import lax
from jax.experimental import pallas as pl
from jax.experimental.pallas import tpu as pltpu
from jax.sharding import PartitionSpec as P

HEADS = 16
EPS = 1e-06
SMOOTH = 0.01
MESH = pl.DeviceIdType.MESH
F32 = jnp.float32
BF16 = jnp.bfloat16


def flip1(p):
    return p + 1 - 2 * (p % 2)


def flip3(p):
    return 3 - p


def coordinates():
    ens, space = lax.axis_index("ens"), lax.axis_index("space")
    z = (space // 8) * 4 + ens // 4
    return (space // 2) % 4, ens % 4, z, space % 2


def device(x, y, z, core):
    return ((z % 4) * 4 + y, (z // 4) * 8 + x * 2 + core)


def remote(src, dst, sems, target):
    return pltpu.make_async_remote_copy(
        src_ref=src,
        dst_ref=dst,
        send_sem=sems[0],
        recv_sem=sems[1],
        device_id=target,
        device_id_type=MESH,
    )


def greet(targets):
    barrier = pltpu.get_barrier_semaphore()
    for target in targets:
        pl.semaphore_signal(barrier, inc=1, device_id=target, device_id_type=MESH)
    pl.semaphore_wait(barrier, len(targets))


def score_kernel(
    channels, points_all, field_ref, target_ref, slopes_ref, loss_ref, seen, out, ssem, rsem, bsem, csem
):
    ens, space = lax.axis_index("ens"), lax.axis_index("space")
    others = [(ens + d) % 16 for d in range(1, 16)]
    greet([(o, space) for o in others])
    sends = []
    for d, o in enumerate(others):
        copy = remote(field_ref.at[o], seen.at[ens], (ssem.at[d], rsem.at[d]), (o, space))
        copy.start()
        sends.append(copy)
    seen[ens] = field_ref[ens]
    for copy in sends:
        copy.wait()
    weight = (channels * points_all) ** (-0.5)
    pair_weight = 1.0 / (16 * 15)
    fields = [seen[m] for m in range(16)]
    truth = target_ref[ens]
    slope_sums = [jnp.zeros((8, 128), F32) for _ in range(16)]
    spread = jnp.zeros((8, 128), F32)
    for m in range(16):
        for k in range(m):
            apart = fields[m] - fields[k]
            square = apart * apart + SMOOTH
            inverse = lax.rsqrt(square)
            spread = spread + square * inverse
            tilt = apart * inverse
            slope_sums[m] = slope_sums[m] + tilt
            slope_sums[k] = slope_sums[k] - tilt
    skill = jnp.zeros((8, 128), F32)
    for m in range(16):
        apart = fields[m] - truth
        square = apart * apart + SMOOTH
        inverse = lax.rsqrt(square)
        skill = skill + square * inverse
        out[m] = weight * (apart * inverse * (1.0 / 16) - pair_weight * slope_sums[m])
    total = weight * (skill * (1.0 / 16) - pair_weight * spread)
    row = ens * 8 + lax.broadcasted_iota(jnp.int32, (8, 128), 0)
    total = jnp.where(row < channels, total, 0.0)
    loss_ref[...] = total
    backs = []
    for d, o in enumerate(others):
        copy = remote(out.at[o], slopes_ref.at[ens], (bsem.at[d], csem.at[d]), (o, space))
        copy.start()
        backs.append(copy)
    slopes_ref[ens] = out[ens]
    for copy in backs:
        copy.wait()


def score(field, target, channels, points_all):
    whole = pl.BlockSpec(memory_space=pltpu.VMEM)
    return pl.pallas_call(
        functools.partial(score_kernel, channels, points_all),
        out_shape=(
            jax.ShapeDtypeStruct((16, 8, 128), F32),
            jax.ShapeDtypeStruct((8, 128), F32),
        ),
        in_specs=[whole] * 2,
        out_specs=(whole, whole),
        scratch_shapes=[pltpu.VMEM((16, 8, 128), F32), pltpu.VMEM((16, 8, 128), F32)]
        + [pltpu.SemaphoreType.DMA((15,))] * 4,
        compiler_params=pltpu.CompilerParams(collective_id=1, has_side_effects=True),
        name="score",
    )(field, target)


def across(left, right):
    return lax.dot_general(left, right, (((0,), (0,)), ((), ())), preferred_element_type=F32)


def total_kernel(
    channels,
    acts_ref, parts_ref, slopes_ref, normed_ref, loss_ref,
    loss_out, out_out, query_out, key_out, value_out, mix_out,
    acts_in, parts_in, work, r1, r2, r3, r4, last, rz,
    halves, half_in, half_sum, g1, own2, g2, own3, g3, g4,
    pair_s, pair_r, s1, q1, s2, q2, s3, q3, s4, q4, zs, zr,
    as1, ar1, as2, ar2, as3, ar3,
):
    x, y, z, core = coordinates()
    ens, space = lax.axis_index("ens"), lax.axis_index("space")
    partner = device(x, y, z, 1 - core)
    ens_others = [((ens + d) % 16, space) for d in range(1, 16)]
    spot = space // 2
    space_others = [(ens, ((spot + d) % 8) * 2 + core) for d in range(1, 8)]
    z_others = [device(x, y, (z + d) % 8, core) for d in range(1, 8)]
    zl, zh = z % 4, z // 4
    z_only = [device(x, y, (1 - zh) * 4 + (zl + d) % 4, core) for d in range(1, 4)]
    greet([partner] + ens_others + space_others + z_only)

    pending = []

    def send(src, dst, sems, target):
        copy = remote(src, dst, sems, target)
        copy.start()
        pending.append(copy)
        return copy

    pair = [send(acts_ref.at[i], acts_in.at[i], (pair_s.at[i], pair_r.at[i]), partner) for i in range(3)]
    pair += [
        send(parts_ref.at[i, 1 - core], parts_in.at[i], (pair_s.at[3 + i], pair_r.at[3 + i]), partner)
        for i in range(2)
    ]
    readout = jnp.dot(slopes_ref[...], normed_ref[...], preferred_element_type=F32)
    rows = lax.broadcasted_iota(jnp.int32, (128, 512), 0)
    lanes = lax.broadcasted_iota(jnp.int32, (128, 512), 1)
    loss = jnp.sum(loss_ref[...])
    high = loss.astype(BF16).astype(F32)
    for h in range(2):
        mine = jnp.where(core == h, 1.0, 0.0)
        part = jnp.where(rows < channels, readout[:, 512 * h : 512 * h + 512], 0.0)
        note = jnp.where(lanes == 0, high, jnp.where(lanes == 1, loss - high, 0.0)) * mine
        part = jnp.where(rows == channels, note, part)
        halves[h] = part.astype(BF16).reshape(16, 8, 512)
    pair.append(send(halves.at[1 - core], half_in, (pair_s.at[5], pair_r.at[5]), partner))
    pair[5].wait_recv()
    half_sum[...] = (halves[core].astype(F32) + half_in[...].astype(F32)).astype(BF16)
    gather1 = [
        send(half_sum.at[t[0]], g1.at[d], (as1.at[d], ar1.at[d]), t) for d, t in enumerate(ens_others)
    ]
    for copy in pair[:5]:
        copy.wait_recv()

    lane = lax.broadcasted_iota(jnp.int32, (1024, 256), 1) % 128

    def products(step, carry):
        at = pl.multiple_of(step * 256, 256)
        mine = [parts_ref[i, core, :, pl.ds(at, 256)] for i in range(2)]
        theirs = [parts_in[i, :, pl.ds(at, 256)] for i in range(2)]
        node = across(acts_ref[0], mine[0]) + across(acts_in[0], theirs[0])
        grid = across(acts_ref[1], mine[1]) + across(acts_in[1], theirs[1])
        mixed = across(acts_ref[2], mine[1]) + across(acts_in[2], theirs[1])
        found = (node.astype(BF16), jnp.where(lane < 64, grid, mixed).astype(BF16))
        for j in range(2):
            column = step * 2 + j
            cz, cx = column // 4, column % 4
            for e in range(16):
                for r in range(2):
                    at_row = e * 64 + r * 32
                    block0 = found[0][at_row : at_row + 32, 128 * j : 128 * j + 128]
                    block1 = found[1][at_row : at_row + 32, 128 * j : 128 * j + 128]
                    work[r, cx, e % 4, cz * 4 + e // 4] = block0
                    work[2 + r, e % 4, cx, cz * 4 + e // 4] = block1
        return carry

    lax.fori_loop(0, 4, products, 0)

    def beside(c, axis, value):
        along_x = (c < 2) == (axis == 0)
        return device(value, y, z, core) if along_x else device(x, value, z, core)

    flips = [(flip1, flip3), (flip3, flip1)] * 2
    places = [(x, y), (x, y), (y, x), (y, x)]
    first, second, third, fourth = {}, {}, {}, {}
    for c in range(4):
        f1, f2 = flips[c]
        p, q = places[c]
        for slot, block in ((1, f2(f1(p))), (0, f1(p))):
            first[c, slot] = send(
                work.at[c, block], r1.at[c, slot], (s1.at[c, slot], q1.at[c, slot]), beside(c, 0, f1(p))
            )
    for c in range(4):
        f1, f2 = flips[c]
        p, q = places[c]
        first[c, 1].wait_recv()
        work[c, f2(p)] = (work[c, f2(p)].astype(F32) + r1[c, 1].astype(F32)).astype(BF16)
        second[c] = send(work.at[c, f2(p)], r2.at[c], (s2.at[c], q2.at[c]), beside(c, 0, f2(p)))

    for copy in gather1:
        copy.wait_recv()
    summed = half_sum[ens].astype(F32)
    for d in range(15):
        summed = summed + g1[d].astype(F32)
    own2[...] = summed.astype(BF16)
    gather2 = [send(own2, g2.at[d], (as2.at[d], ar2.at[d]), t) for d, t in enumerate(space_others)]

    def both(c, p, at):
        return work[c, p, at].astype(F32) + r1[c, 0, at].astype(F32) + r2[c, at].astype(F32)

    for c in range(4):
        f1, f2 = flips[c]
        p, q = places[c]
        first[c, 0].wait_recv()
        second[c].wait_recv()
        for slot, block in ((1, f2(f1(q))), (0, f1(q))):
            work[c, p, block] = both(c, p, block).astype(BF16)
            third[c, slot] = send(
                work.at[c, p, block], r3.at[c, slot], (s3.at[c, slot], q3.at[c, slot]), beside(c, 1, f1(q))
            )

    for copy in gather2:
        copy.wait_recv()
    summed = own2[...].astype(F32)
    for d in range(7):
        summed = summed + g2[d].astype(F32)
    own3[...] = summed.astype(BF16)
    gather3 = [
        send(own3, g3.at[ens], (as3.at[d], ar3.at[d]), t) for d, t in enumerate(ens_others)
    ]
    g3[ens] = own3[...]

    for c in range(4):
        f1, f2 = flips[c]
        p, q = places[c]
        third[c, 1].wait_recv()
        work[c, p, f2(q)] = (both(c, p, f2(q)) + r3[c, 1].astype(F32)).astype(BF16)
        fourth[c] = send(work.at[c, p, f2(q)], r4.at[c], (s4.at[c], q4.at[c]), beside(c, 1, f2(q)))
    for c in range(4):
        p, q = places[c]
        third[c, 0].wait_recv()
        fourth[c].wait_recv()
        block = both(c, p, q) + r3[c, 0].astype(F32) + r4[c].astype(F32)
        block = block.astype(BF16)
        for k in range(8):
            last[k, c] = block[k]
    deep = [
        send(last.at[(z + d + 1) % 8], rz.at[d], (zs.at[d], zr.at[d]), t) for d, t in enumerate(z_others)
    ]

    for copy in gather3:
        copy.wait_recv()
    final = send(g3, g4, (pair_s.at[6], pair_r.at[6]), partner)
    final.wait_recv()
    here = g3[...].astype(F32).reshape(128, 512)
    there = g4[...].astype(F32).reshape(128, 512)
    low = jnp.where(core == 0, here, there)
    upper = jnp.where(core == 0, there, here)
    out_out[:, 0:512] = low[:channels]
    out_out[:, 512:1024] = upper[:channels]
    notes = jnp.where(lanes < 2, low + upper, 0.0)
    loss_out[...] = jnp.full((8, 128), jnp.sum(jnp.where(rows == channels, notes, 0.0)))

    for copy in deep:
        copy.wait_recv()
    grads = last[z].astype(F32)
    for d in range(7):
        grads = grads + rz[d].astype(F32)
    for r in range(2):
        key_out[32 * r : 32 * r + 32, :] = grads[r][:, 0:64]
        value_out[32 * r : 32 * r + 32, :] = grads[r][:, 64:128]
        query_out[32 * r : 32 * r + 32, :] = grads[2 + r][:, 0:64]
        mix_out[32 * r : 32 * r + 32, :] = grads[2 + r][:, 64:128]
    for copy in pending:
        copy.wait_send()


def totals(acts, parts, slopes, normed, loss, channels):
    whole = pl.BlockSpec(memory_space=pltpu.VMEM)
    dma = pltpu.SemaphoreType.DMA
    square = jax.ShapeDtypeStruct((64, 64), F32)
    return pl.pallas_call(
        functools.partial(total_kernel, channels),
        out_shape=(
            jax.ShapeDtypeStruct((8, 128), F32),
            jax.ShapeDtypeStruct((channels, 1024), F32),
            square, square, square, square,
        ),
        in_specs=[whole] * 5,
        out_specs=(whole,) * 6,
        scratch_shapes=[
            pltpu.VMEM((3, 128, 1024), BF16),
            pltpu.VMEM((2, 128, 1024), BF16),
            pltpu.VMEM((4, 4, 4, 8, 32, 128), BF16),
            pltpu.VMEM((4, 2, 4, 8, 32, 128), BF16),
            pltpu.VMEM((4, 4, 8, 32, 128), BF16),
            pltpu.VMEM((4, 2, 8, 32, 128), BF16),
            pltpu.VMEM((4, 8, 32, 128), BF16),
            pltpu.VMEM((8, 4, 32, 128), BF16),
            pltpu.VMEM((7, 4, 32, 128), BF16),
            pltpu.VMEM((2, 16, 8, 512), BF16),
            pltpu.VMEM((16, 8, 512), BF16),
            pltpu.VMEM((16, 8, 512), BF16),
            pltpu.VMEM((15, 8, 512), BF16),
            pltpu.VMEM((8, 512), BF16),
            pltpu.VMEM((7, 8, 512), BF16),
            pltpu.VMEM((8, 512), BF16),
            pltpu.VMEM((16, 8, 512), BF16),
            pltpu.VMEM((16, 8, 512), BF16),
            dma((7,)), dma((7,)),
            dma((4, 2)), dma((4, 2)), dma((4,)), dma((4,)),
            dma((4, 2)), dma((4, 2)), dma((4,)), dma((4,)),
            dma((7,)), dma((7,)),
            dma((15,)), dma((15,)), dma((7,)), dma((7,)), dma((15,)), dma((15,)),
        ],
        compiler_params=pltpu.CompilerParams(
            collective_id=2, has_side_effects=True, vmem_limit_bytes=48 << 20
        ),
        name="totals",
    )(acts, parts, slopes, normed, loss)


def with_halo(value, sides, width):
    for axis, dim in sides:
        size, length = (lax.axis_size(axis), value.shape[dim])
        up = [(i, (i + 1) % size) for i in range(size)]
        down = [(j, i) for i, j in up]
        last = lax.slice_in_dim(value, length - width, length, axis=dim)
        leading = lax.slice_in_dim(value, 0, width, axis=dim)
        before = lax.ppermute(last, axis, up)
        after = lax.ppermute(leading, axis, down)
        value = jnp.concatenate([before, value, after], axis=dim)
    return value


def by_heads(v):
    return v.reshape(v.shape[0], HEADS, v.shape[1] // HEADS)


def dot32(left, right):
    return jnp.dot(left, right, preferred_element_type=F32)


def columns(left, right):
    return lax.dot_general(left, right, (((1,), (1,)), ((), ())), preferred_element_type=F32)


def body(
    grid_hidden, latent, tile_neighbor_index, target, w_query, w_key, w_value, w_mix, readout_weight
):
    node_count, features = latent.shape[1], latent.shape[2]
    shards = lax.axis_size("space")
    shard_index = lax.axis_index("space")
    channels, points = target.shape
    rimmed = with_halo(latent, (("space", 1),), node_count)
    positions = jnp.mod(
        tile_neighbor_index[0] - (shard_index - 1) * node_count, node_count * shards
    )
    nodes = jnp.take(rimmed[0], positions, axis=0)
    grid = grid_hidden[0]
    factor = (features // HEADS) ** (-0.5)
    readout = jnp.pad(readout_weight, ((0, 128 - channels), (0, 0)))
    truth = jnp.pad(target, ((0, 128 - channels), (0, 0))).reshape(16, 8, points)

    queries = dot32(grid, w_query).astype(BF16)
    keyset = dot32(nodes, w_key).astype(BF16)
    valueset = dot32(nodes, w_value).astype(BF16)

    def einsum(spec, a, b):
        return jnp.einsum(spec, a, b, preferred_element_type=F32)

    scores = einsum("qhd,khd->hqk", by_heads(queries), by_heads(keyset)) * factor
    raised = jnp.exp(scores - jnp.max(scores, axis=-1, keepdims=True))
    softmaxed = raised / jnp.sum(raised, axis=-1, keepdims=True)
    softmaxed_b = softmaxed.astype(BF16)
    attended = einsum("hqk,khd->qhd", softmaxed_b, by_heads(valueset))
    attended = attended.reshape(points, features).astype(BF16)
    hidden = grid.astype(F32) + dot32(attended, w_mix)
    inverse = lax.rsqrt(jnp.mean(hidden * hidden, axis=-1, keepdims=True) + EPS)
    normed = hidden * inverse
    normed_b = normed.astype(BF16)
    field = columns(readout, normed_b).reshape(16, 8, points)

    slopes, loss_part = score(field, truth, channels, points * shards)
    slopes_b = slopes.reshape(128, points).astype(BF16)

    d_normed = lax.dot_general(
        slopes_b, readout, (((0,), (0,)), ((), ())), preferred_element_type=F32
    )
    d_hidden = inverse * (d_normed - normed * jnp.mean(d_normed * normed, axis=-1, keepdims=True))
    d_hidden_b = d_hidden.astype(BF16)
    d_attended = columns(d_hidden_b, w_mix).astype(BF16)
    d_probs = einsum("qhd,khd->hqk", by_heads(d_attended), by_heads(valueset))
    d_values = einsum("hqk,qhd->khd", softmaxed_b, by_heads(d_attended)).astype(BF16)
    d_scores = softmaxed * (d_probs - jnp.sum(d_probs * softmaxed, axis=-1, keepdims=True)) * factor
    d_scores_b = d_scores.astype(BF16)
    d_queries = einsum("hqk,khd->qhd", d_scores_b, by_heads(keyset)).astype(BF16)
    d_keys = einsum("hqk,qhd->khd", d_scores_b, by_heads(queries)).astype(BF16)

    def by_parity(a, b):
        both = jnp.stack([a.reshape(points, 8, 2, 64), b.reshape(points, 8, 2, 64)], axis=3)
        return both.transpose(2, 0, 1, 3, 4).reshape(2, points, features)

    parts = jnp.stack([by_parity(d_keys, d_values), by_parity(d_queries, by_heads(d_hidden_b))])
    acts = jnp.stack([nodes, grid, attended])
    loss, grad_out, grad_query, grad_key, grad_value, grad_mix = totals(
        acts, parts, slopes_b, normed_b, loss_part, channels
    )
    return loss[0, 0], grad_out, grad_query, grad_key, grad_value, grad_mix


def solution(mesh):
    in_specs = (
        P("ens", "space", None),
        P("ens", "space", None),
        P("space", None),
        P(None, "space"),
        P(), P(), P(), P(), P(),
    )
    out_specs = (
        P(), P(),
        P("ens", "space"), P("ens", "space"), P("ens", "space"), P("ens", "space"),
    )
    return jax.shard_map(body, mesh=mesh, in_specs=in_specs, out_specs=out_specs, check_vma=False)
```

time: 402 us -> 124 us (0.31)
  waiting for transfers between devices: 298 us -> 1.01 us
  Pallas kernels: 0 us -> 73.8 us
  between operations: 17.1 us -> 0.96 us
  local copies, waits for them, and re-layouts: 26.1 us -> 13.2 us
  blocking collectives: 10.7 us -> 0 us
  starting transfers between devices: 7.98 us -> 1.82 us
  matrix products: 30 us -> 24.8 us
    psum x1 -> x0, waiting for transfers between devices: 177 us -> none  [packed_total(): subtotal = lax.psum(line, axis)]
    unnamed x4 -> x0, waiting for transfers between devices: 109 us -> none
    pallas_call x0 -> x2, Pallas kernels: none -> 73.8 us  [the longest x1 55.4 us: totals(): pl.pallas_call(functools.partial(total_kernel, channels), out_shape=(jax....]
    unnamed x33 -> x39, local copies, waits for them, and re-layouts: 15.2 us -> 4.33 us
    all_to_all x1 -> x0, blocking collectives: 10.7 us -> none  [body(): lax.all_to_all(member_slopes.astype(jnp.bfloat16), 'ens', split_axis=0, c...]
    all_to_all x1 -> x0, waiting for transfers between devices: 7.4 us -> none  [body(): lax.all_to_all(member_own_field, 'ens', split_axis=2, concat_axis=0, tile...]
    concatenate x3 -> x0, other arithmetic: 6.07 us -> none  [the longest x2 5.14 us: sent_together(): both = jnp.concatenate(arrays, axis=along)]
    all_to_all x1 -> x0, starting transfers between devices: 6.04 us -> none  [body(): lax.all_to_all(member_own_field, 'ens', split_axis=2, concat_axis=0, tile...]
  transfers between devices with their start and end apart: 6 -> 2, of which waited for: 5 -> 1; matrix products, arithmetic and copies ran while one was open for 3% -> 4% of each run, Pallas kernels for 0% -> 0%
where the time goes in v1:
time: 124 us; the launch traced here: 122 us
  Pallas kernels  73.8 us (60%)
  matrix products  24.8 us (20%)
  local copies, waits for them, and re-layouts  13.2 us (11%)
  other arithmetic  6.41 us (5%)
  starting transfers between devices  1.82 us (1%)
    pallas_call x1, Pallas kernels, totals(): pl.pallas_call(functools.partial(total_kernel, channels), out_shape=(jax....  55.4 us
    pallas_call x1, Pallas kernels, score(): pl.pallas_call(functools.partial(score_kernel, channels, points_all), out...  18.4 us
    dot_general x5, matrix products, einsum(): return jnp.einsum(spec, a, b, preferred_element_type=F32)  13.4 us
    dot_general x4, matrix products, dot32(): return jnp.dot(left, right, preferred_element_type=F32)  6.94 us
    unnamed x39, local copies, waits for them, and re-layouts  4.33 us
  transfers between devices with their start and end apart: 2, of which 1 were waited for; matrix products, arithmetic and copies ran while one was open for 4% of the time, Pallas kernels for 0%

profile of v1, /device:TPU:6, one launch (start us, length us, event | category | flops | bytes accessed | tf_op | source)
XLA Modules:
  0.0 122.0 jit_solution(17262224065324648934)
XLA Ops:
  0.6 0.0 copy-start
  0.7 0.1 collective-permute-start
  0.8 1.7 %collective-permute-start.1 = (bf16[1,128,1024]{2,1,0:T(8,128)(2,1)}, bf16[1,128,1024]{2,1,0:T(8,128)(2,1)}, u32[]{:S(2)}, u32[]{:S(2)}) collective-permute-start(bf16[1,128,1024]{2,1,0:T(8,128)(2,1)} %param.10), channel_id=1, source_target_pairs={{1,0},{2,1},{3,2},{4,3},{5,4},{6,5},{7,6},{8,7},{9,8},{10,9},{11,1... | collective-permute-start | bytes 786440 | tf_op jit(solution)/shard_map/ppermute | solution.py:354
  2.5 1.4 %pad_bitcast_fusion.target_ref = f32[16,8,128]{2,1,0:T(8,128)} fusion(f32[100,128]{1,0:T(8,128)} %param.12), kind=kLoop, calls=%fused_computation.43 | loop fusion | bytes 116736 | tf_op jit(solution)/shard_map/reshape | solution.py:386
  3.9 0.7 fusion.22
  4.6 2.1 %convolution_convert_fusion.6 = bf16[128,1024]{1,0:T(8,128)(2,1)S(1)} fusion(bf16[1024,1024]{1,0:T(8,128)(2,1)} %param.13, bf16[1,128,1024]{2,1,0:T(8,128)(2,1)} %param.9), kind=kOutput, calls=%fused_computation.17 | convolution fusion | flops 268566528 | bytes 2621440 | tf_op jit(solution)/shard_map/dot_general | solution.py:364
  6.7 0.9 copy.33
  7.6 0.7 copy-done.14
  8.3 1.0 collective-permute-done.1
  9.3 1.1 maximum_bitcast_fusion
  10.4 0.9 gather_fusion
  11.3 2.1 %convolution_convert_fusion.5 = bf16[128,1024]{1,0:T(8,128)(2,1)S(1)} fusion(bf16[1024,1024]{1,0:T(8,128)(2,1)} %param.14, bf16[128,1024]{1,0:T(8,128)(2,1)S(1)} %gather_fusion, pred[128]{0:T(512)(128)(4,1)S(1)} %compare_and_fusion), kind=kOutput, calls=%fused_computation.16 | convolution fusion | flops 268697600 | bytes 2621568 | tf_op jit(solution)/shard_map/dot_general | solution.py:364
  13.4 0.2 copy.34
  13.6 2.2 %convolution_convert_fusion.7 = bf16[128,1024]{1,0:T(8,128)(2,1)S(1)} fusion(bf16[1024,1024]{1,0:T(8,128)(2,1)} %param.15, bf16[128,1024]{1,0:T(8,128)(2,1)S(1)} %gather_fusion, pred[128]{0:T(512)(128)(4,1)S(1)} %compare_and_fusion), kind=kOutput, calls=%fused_computation.18 | convolution fusion | flops 268697600 | bytes 2621568 | tf_op jit(solution)/shard_map/dot_general | solution.py:364
  15.8 0.2 copy.32
  15.9 1.5 %fusion.33 = (f32[16,128]{1,0:T(8,128)S(1)}, f32[16,128,128]{1,2,0:T(8,128)}) fusion(bf16[128,16,64]{0,2,1:T(8,128)(2,1)S(1)} %bitcast.77, bf16[128,16,64]{0,2,1:T(8,128)(2,1)S(1)} %bitcast.80), kind=kOutput, calls=%fused_computation.70 | convolution fusion | flops 34340992 | bytes 1581056 | tf_op jit(solution)/shard_map/sub | solution.py:396
  17.4 1.7 %convolution_convert_fusion.4 = bf16[16,64,128]{2,1,0:T(8,128)(2,1)S(1)} fusion(bf16[128,16,64]{0,2,1:T(8,128)(2,1)S(1)} %bitcast.69, f32[16,128]{1,0:T(8,128)S(1)} %get-tuple-element.22, bf16[128,16,64]{0,2,1:T(8,128)(2,1)S(1)} %bitcast.78, bf16[128,16,64]{0,2,1:T(8,128)(2,1)} %bitcast.81), kind=kOutput, calls=%fused_computation.15 | convolution fusion | flops 68290688 | bytes 1056768 | tf_op jit(solution)/shard_map/hqk,khd->qhd/dot_general | solution.py:393
  19.1 0.0 copy-done.4
  19.2 0.5 multiply_reduce_fusion.2
  19.8 0.1 multiply_convert_fusion.1.normed_ref
  19.9 0.3 copy-done.8
  20.2 0.9 convolution_bitcast_fusion.field_ref
  21.0 18.4 %score.1 = (f32[16,8,128]{2,1,0:T(8,128)}, f32[8,128]{1,0:T(8,128)}) custom-call(f32[16,8,128]{2,1,0:T(8,128)} %convolution_bitcast_fusion.field_ref, f32[16,8,128]{2,1,0:T(8,128)} %pad_bitcast_fusion.target_ref), custom_call_target="tpu_custom_call" | custom-call | tf_op jit(solution)/shard_map/score/pallas_call | solution.py:106
  39.4 0.8 convert_bitcast_fusion.slopes_ref
  40.3 1.3 %multiply_reduce_fusion.1 = (f32[128]{0:T(128)S(1)}, f32[128,1024]{1,0:T(8,128)S(1)}) fusion(f32[128,1024]{1,0:T(8,128)S(1)} %get-tuple-element.25, f32[128]{0:T(128)S(1)} %add_rsqrt_fusion, bf16[128,128]{1,0:T(8,128)(2,1)S(1)} %convert_bitcast_fusion.slopes_ref, bf16[100,1024]{1,0:T(8,128)(2,1)} %param.17), kind=kOutput, calls=%fused_computation.29 | convolution fusion | flops 33947520 | bytes 1287168 | tf_op jit(solution)/shard_map/dot_general | solution.py:410
  41.6 0.2 multiply_convert_fusion
  41.7 0.8 convolution_convert_fusion.3
  42.6 0.9 copy.37
  43.4 2.3 %fusion.34 = f32[16,128,128]{1,2,0:T(8,128)} fusion(bf16[128,16,64]{0,2,1:T(8,128)(2,1)} %bitcast.72, bf16[128,16,64]{0,2,1:T(8,128)(2,1)S(1)} %bitcast.70), kind=kOutput, calls=%fused_computation.71 | convolution fusion | flops 33554432 | bytes 1572864 | tf_op jit(solution)/shard_map/qhd,khd->hqk/dot_general | solution.py:393
  45.8 2.6 %convolution_convert_fusion.1 = bf16[16,64,128]{2,1,0:T(8,128)(2,1)} fusion(bf16[128,16,64]{0,2,1:T(8,128)(2,1)} %bitcast.73, f32[16,128]{1,0:T(8,128)S(1)} %get-tuple-element.22, bf16[128,16,64]{0,2,1:T(8,128)(2,1)} %bitcast.76, bf16[128,16,64]{0,2,1:T(8,128)(2,1)} %bitcast.82), kind=kOutput, calls=%fused_computation.12 | convolution fusion | flops 68290688 | bytes 1056768 | tf_op jit(solution)/shard_map/hqk,qhd->khd/dot_general | solution.py:393
  48.4 3.4 %convolution_convert_fusion.2 = bf16[16,64,128]{2,1,0:T(8,128)(2,1)} fusion(bf16[128,16,64]{0,2,1:T(8,128)(2,1)S(1)} %bitcast.79, f32[16,128,128]{1,2,0:T(8,128)} %fusion.34, f32[16,128,128]{1,2,0:T(8,128)} %get-tuple-element.23, f32[16,128]{1,0:T(8,128)S(1)} %get-tuple-element.22), kind=kOutput, calls=%fused_computation.13 | convolution fusion | flops 35522688 | bytes 2629632 | tf_op jit(solution)/shard_map/hqk,qhd->khd/dot_general | solution.py:393
  51.8 3.4 %convolution_convert_fusion = bf16[16,64,128]{2,1,0:T(8,128)(2,1)} fusion(bf16[128,16,64]{0,2,1:T(8,128)(2,1)S(1)} %bitcast.83, f32[16,128,128]{1,2,0:T(8,128)} %fusion.34, f32[16,128,128]{1,2,0:T(8,128)} %get-tuple-element.23, f32[16,128]{1,0:T(8,128)S(1)} %get-tuple-element.22), kind=kOutput, calls=%fused_computation.11 | convolution fusion | flops 35522688 | bytes 2629632 | tf_op jit(solution)/shard_map/hqk,khd->qhd/dot_general | solution.py:393
  55.2 0.8 copy.43
  56.0 0.1 bitcast_select_fusion
  56.2 1.0 pad_maximum_fusion.2
  57.3 1.0 copy.45
  58.3 1.0 maximum_bitcast_fusion.1
  59.3 1.0 copy.46
  60.3 1.1 copy.36
  61.4 1.3 %pad_maximum_fusion.parts_ref = bf16[2,2,128,1024]{3,2,1,0:T(8,128)(2,1)S(1)} fusion(bf16[1,2,128,1024]{3,2,1,0:T(8,128)(2,1)} %copy.46, bf16[1,2,128,1024]{3,2,1,0:T(8,128)(2,1)} %copy.45), kind=kLoop, calls=%fused_computation.20 | loop fusion | flops 524288 | bytes 2097152 | tf_op jit(solution)/shard_map/stack | solution.py:427
  62.7 0.1 pad_maximum_fusion.1.acts_ref
  62.9 55.4 %totals.1 = (f32[8,128]{1,0:T(8,128)S(1)}, f32[100,1024]{1,0:T(8,128)S(1)}, f32[64,64]{1,0:T(8,128)S(1)}, f32[64,64]{1,0:T(8,128)S(1)}, f32[64,64]{1,0:T(8,128)S(1)}, /*index=5*/f32[64,64]{1,0:T(8,128)S(1)}) custom-call(bf16[3,128,1024]{2,1,0:T(8,128)(2,1)S(1)} %pad_maximum_fusion.1.acts_ref, bf16[2,2,128,1024]{3,2,1,0:T(8,128)(2,1)S(1)} %pad_maximum_fusion.parts_ref, ...), custom_call_target="tpu_custom_call" | custom-call | tf_op jit(solution)/shard_map/totals/pallas_call | solution.py:305
  118.2 0.5 slice.3
  118.8 0.8 copy.57
  119.5 0.6 copy.58
  120.1 0.6 copy.59
  120.7 0.6 copy.60
  121.4 0.6 copy.61
  (37 shorter events, 0.2 us)
Async XLA Ops:
  0.6 18.5 %copy-start = (bf16[1024,1024]{1,0:T(8,128)(2,1)S(1)}, bf16[1024,1024]{1,0:T(8,128)(2,1)}, u32[]{:S(2)}) copy-start(bf16[1024,1024]{1,0:T(8,128)(2,1)} %param.16) | copy-start | bytes 6291460
  0.6 8.7 %copy-start.13 = (bf16[1,128,1024]{2,1,0:T(8,128)(2,1)S(1)}, bf16[1,128,1024]{2,1,0:T(8,128)(2,1)}, u32[]{:S(2)}) copy-start(bf16[1,128,1024]{2,1,0:T(8,128)(2,1)} %param.10) | copy-start | bytes 786436
  0.7 6.9 %copy-start.16 = (s32[1,128]{1,0:T(1,128)S(1)}, s32[1,128]{1,0:T(1,128)}, u32[]{:S(2)}) copy-start(s32[1,128]{1,0:T(1,128)} %param.11) | copy-start | bytes 1540
  0.7 7.0 %collective-permute-start = (bf16[1,128,1024]{2,1,0:T(8,128)(2,1)}, bf16[1,128,1024]{2,1,0:T(8,128)(2,1)S(1)}, u32[]{:S(2)}, u32[]{:S(2)}) collective-permute-start(bf16[1,128,1024]{2,1,0:T(8,128)(2,1)} %param.10), channel_id=1, source_target_pairs={{0,1},{1,2},{2,3},{3,4},{4,5},{5,6},{6,7},{7,8},{8,9},{9,10},{10,1... | collective-permute-start | bytes 786440 | tf_op jit(solution)/shard_map/ppermute | solution.py:353
  0.8 8.6 %collective-permute-start.1 = (bf16[1,128,1024]{2,1,0:T(8,128)(2,1)}, bf16[1,128,1024]{2,1,0:T(8,128)(2,1)}, u32[]{:S(2)}, u32[]{:S(2)}) collective-permute-start(bf16[1,128,1024]{2,1,0:T(8,128)(2,1)} %param.10), channel_id=1, source_target_pairs={{1,0},{2,1},{3,2},{4,3},{5,4},{6,5},{7,6},{8,7},{9,8},{10,9},{11,1... | collective-permute-start | bytes 786440 | tf_op jit(solution)/shard_map/ppermute | solution.py:354
  7.6 0.7 copy-start.14
  13.4 2.6 %copy-start.9 = (bf16[128,1024]{0,1:T(8,128)(2,1)S(1)}, bf16[128,1024]{0,1:T(8,128)(2,1)}, u32[]{:S(2)}) copy-start(bf16[128,1024]{0,1:T(8,128)(2,1)} %copy.33) | copy-start | bytes 786436
  13.6 3.9 %copy-start.11 = (bf16[128,1024]{0,1:T(8,128)(2,1)}, bf16[128,1024]{0,1:T(8,128)(2,1)S(1)}, u32[]{:S(2)}) copy-start(bf16[128,1024]{0,1:T(8,128)(2,1)S(1)} %copy.34) | copy-start | bytes 786436
  15.9 3.2 %copy-start.4 = (bf16[128,1024]{0,1:T(8,128)(2,1)}, bf16[128,1024]{0,1:T(8,128)(2,1)S(1)}, u32[]{:S(2)}) copy-start(bf16[128,1024]{0,1:T(8,128)(2,1)S(1)} %copy.32) | copy-start | bytes 786436
  17.4 1.7 %copy-start.2 = (bf16[1,128,1024]{2,1,0:T(8,128)(2,1)S(1)}, bf16[1,128,1024]{2,1,0:T(8,128)(2,1)}, u32[]{:S(2)}) copy-start(bf16[1,128,1024]{2,1,0:T(8,128)(2,1)} %param.9) | copy-start | bytes 786436
  19.2 1.9 %copy-start.7 = (bf16[16,64,128]{2,1,0:T(8,128)(2,1)}, bf16[16,64,128]{2,1,0:T(8,128)(2,1)S(1)}, u32[]{:S(2)}) copy-start(bf16[16,64,128]{2,1,0:T(8,128)(2,1)S(1)} %convolution_convert_fusion.4) | copy-start | bytes 786436
  19.2 1.0 copy-start.8
  41.7 1.7 %copy-start.5 = (bf16[128,1024]{0,1:T(8,128)(2,1)S(1)}, bf16[128,1024]{0,1:T(8,128)(2,1)}, u32[]{:S(2)}) copy-start(bf16[128,1024]{0,1:T(8,128)(2,1)} %copy-done.4) | copy-start | bytes 786436
  45.8 2.6 %copy-start.10 = (bf16[128,1024]{0,1:T(8,128)(2,1)S(1)}, bf16[128,1024]{0,1:T(8,128)(2,1)}, u32[]{:S(2)}) copy-start(bf16[128,1024]{0,1:T(8,128)(2,1)} %copy.33) | copy-start | bytes 786436
  48.4 3.4 %copy-start.12 = (bf16[128,1024]{0,1:T(8,128)(2,1)S(1)}, bf16[128,1024]{0,1:T(8,128)(2,1)}, u32[]{:S(2)}) copy-start(bf16[128,1024]{0,1:T(8,128)(2,1)} %copy-done.11) | copy-start | bytes 786436
  51.8 4.3 %copy-start.15 = (bf16[16,64,128]{2,1,0:T(8,128)(2,1)S(1)}, bf16[16,64,128]{2,1,0:T(8,128)(2,1)}, u32[]{:S(2)}) copy-start(bf16[16,64,128]{2,1,0:T(8,128)(2,1)} %convolution_convert_fusion.1) | copy-start | bytes 786436
  56.1 2.1 %copy-start.6 = (bf16[128,1024]{0,1:T(8,128)(2,1)S(1)}, bf16[128,1024]{0,1:T(8,128)(2,1)}, u32[]{:S(2)}) copy-start(bf16[128,1024]{0,1:T(8,128)(2,1)} %copy.43) | copy-start | bytes 786436
  59.3 3.4 %copy-start.3 = (bf16[1,128,1024]{2,1,0:T(8,128)(2,1)S(1)}, bf16[1,128,1024]{2,1,0:T(8,128)(2,1)}, u32[]{:S(2)}) copy-start(bf16[1,128,1024]{2,1,0:T(8,128)(2,1)} %param.9) | copy-start | bytes 786436
  60.3 2.5 %copy-start.1 = (f32[8,128]{1,0:T(8,128)S(1)}, f32[8,128]{1,0:T(8,128)}, u32[]{:S(2)}) copy-start(f32[8,128]{1,0:T(8,128)} %get-tuple-element.15.loss_ref) | copy-start | bytes 12292

commit v2 on v1

v2 whole, which is shorter than its diff:
```python
import functools

import jax
import jax.numpy as jnp
from jax import lax
from jax.experimental import pallas as pl
from jax.experimental.pallas import tpu as pltpu
from jax.sharding import PartitionSpec as P

EPS = 1e-06
SMOOTH = 0.01
MESH = pl.DeviceIdType.MESH
F32 = jnp.float32
BF16 = jnp.bfloat16


def flip1(p):
    return p + 1 - 2 * (p % 2)


def flip3(p):
    return 3 - p


def coordinates():
    ens, space = lax.axis_index("ens"), lax.axis_index("space")
    z = (space // 8) * 4 + ens // 4
    return (space // 2) % 4, ens % 4, z, space % 2


def device(x, y, z, core):
    return ((z % 4) * 4 + y, (z // 4) * 8 + x * 2 + core)


def remote(src, dst, sems, target):
    return pltpu.make_async_remote_copy(
        src_ref=src,
        dst_ref=dst,
        send_sem=sems[0],
        recv_sem=sems[1],
        device_id=target,
        device_id_type=MESH,
    )


def across(left, right):
    return lax.dot_general(left, right, (((0,), (0,)), ((), ())), preferred_element_type=F32)


def columns(left, right):
    return lax.dot_general(left, right, (((1,), (1,)), ((), ())), preferred_element_type=F32)


def dot32(left, right):
    return jnp.dot(left, right, preferred_element_type=F32)


def wide_dot(left, weight_ref, out_ref):
    def chunk(step, carry):
        at = pl.multiple_of(step * 256, 256)
        out_ref[:, pl.ds(at, 256)] = dot32(left, weight_ref[:, pl.ds(at, 256)]).astype(out_ref.dtype)
        return carry

    lax.fori_loop(0, 4, chunk, 0)


def step_kernel(
    channels, points_all,
    grid_ref, latent_ref, index_ref, target_ref, wq_ref, wk_ref, wv_ref, wm_ref, readout_ref,
    grads_ref, g3, g4,
    wq, wk, wv, wm, readout, truth, near, probs, queries, keyset, valueset, hidden, d_hidden, d_attended,
    field, seen, out, slopes,
    acts_ref, parts_ref,
    acts_in, parts_in, work, r1, r2, r3, r4, last, rz,
    halves, half_in, half_sum, g1, own2, g2, own3,
    local, halo_s, halo_r, ssem, rsem, bsem, csem,
    pair_s, pair_r, s1, q1, s2, q2, s3, q3, s4, q4, zs, zr,
    as1, ar1, as2, ar2, as3, ar3,
):
    x, y, z, core = coordinates()
    ens, space = lax.axis_index("ens"), lax.axis_index("space")
    partner = device(x, y, z, 1 - core)
    ens_others = [((ens + d) % 16, space) for d in range(1, 16)]
    spot = space // 2
    space_others = [(ens, ((spot + d) % 8) * 2 + core) for d in range(1, 8)]
    z_others = [device(x, y, (z + d) % 8, core) for d in range(1, 8)]
    zl, zh = z % 4, z // 4
    z_only = [device(x, y, (1 - zh) * 4 + (zl + d) % 4, core) for d in range(1, 4)]
    after = (ens, (space + 1) % 16)
    before = (ens, (space + 15) % 16)
    outside = (ens, (space + 16 + 2 * core - 1) % 16)
    targets = [partner, outside] + ens_others + space_others + z_only
    barrier = pltpu.get_barrier_semaphore()
    for target in targets:
        pl.semaphore_signal(barrier, inc=1, device_id=target, device_id_type=MESH)

    loads = []
    pairs_of = (
        (grid_ref, acts_ref.at[1]), (latent_ref, near.at[1]), (wq_ref, wq), (wk_ref, wk), (wv_ref, wv), (wm_ref, wm),
    )
    for i, (src, dst) in enumerate(pairs_of):
        copy = pltpu.make_async_copy(src, dst, local.at[i])
        copy.start()
        loads.append(copy)
    readout[96:128, :] = jnp.zeros((32, 1024), BF16)
    readout[0:channels, :] = readout_ref[...]
    truth[96:128, :] = jnp.zeros((32, 128), F32)
    truth[0:channels, :] = target_ref[...]
    loads[0].wait()
    loads[1].wait()
    pl.semaphore_wait(barrier, len(targets))

    pending = []

    def send(src, dst, sems, target):
        copy = remote(src, dst, sems, target)
        copy.start()
        pending.append(copy)
        return copy

    halo = [
        send(near.at[1], near.at[0], (halo_s.at[0], halo_r.at[0]), after),
        send(near.at[1], near.at[2], (halo_s.at[1], halo_r.at[1]), before),
    ]
    pair = {}
    pair["grid"] = send(acts_ref.at[1], acts_in.at[1], (pair_s.at[1], pair_r.at[1]), partner)
    loads[2].wait()
    wide_dot(acts_ref[1], wq, queries)
    place = (index_ref[...] - (space - 1) * 128 + 2048) & 2047
    node_id = lax.broadcasted_iota(jnp.int32, (384, 128), 0)
    chosen = jnp.where(node_id == place, 1.0, 0.0).astype(BF16)
    for copy in halo:
        copy.wait_recv()
    for n in range(4):
        cut = slice(256 * n, 256 * n + 256)
        found = sum(across(chosen[128 * i : 128 * i + 128], near[i, :, cut]) for i in range(3))
        acts_ref[0, :, cut] = found.astype(BF16)
    pair["node"] = send(acts_ref.at[0], acts_in.at[0], (pair_s.at[0], pair_r.at[0]), partner)
    loads[3].wait()
    wide_dot(acts_ref[0], wk, keyset)
    loads[4].wait()
    wide_dot(acts_ref[0], wv, valueset)

    early = lax.broadcasted_iota(jnp.int32, (128, 128), 1) < 64

    def apart_heads(v):
        zero = jnp.zeros_like(v)
        return jnp.concatenate([jnp.where(early, v, zero), jnp.where(early, zero, v)], axis=0)

    def attend(h, carry):
        at = pl.ds(pl.multiple_of(h * 128, 128), 128)
        scores = columns(queries[:, at], apart_heads(keyset[:, at])) * 0.125
        halves_of = []
        for i in range(2):
            part = scores[:, 128 * i : 128 * i + 128]
            raised = jnp.exp(part - jnp.max(part, axis=-1, keepdims=True))
            halves_of.append(raised / jnp.sum(raised, axis=-1, keepdims=True))
        soft = jnp.concatenate(halves_of, axis=1)
        probs[h] = soft
        acts_ref[2, :, at] = dot32(soft.astype(BF16), apart_heads(valueset[:, at])).astype(BF16)
        return carry

    lax.fori_loop(0, 8, attend, 0)
    pair["attended"] = send(acts_ref.at[2], acts_in.at[2], (pair_s.at[2], pair_r.at[2]), partner)
    loads[5].wait()
    wide_dot(acts_ref[2], wm, hidden)
    full = hidden[...] + acts_ref[1].astype(F32)
    inverse = lax.rsqrt(jnp.sum(full * full, axis=-1, keepdims=True) * (1.0 / 1024) + EPS)
    hidden[...] = full * inverse
    normed_b = hidden[...].astype(BF16)
    field[...] = columns(readout[...], normed_b).reshape(16, 8, 128)

    sends = [
        send(field.at[t[0]], seen.at[ens], (ssem.at[d], rsem.at[d]), t) for d, t in enumerate(ens_others)
    ]
    seen[ens] = field[ens]
    for copy in sends:
        copy.wait_recv()
    weight = (channels * points_all) ** (-0.5)
    pair_weight = 1.0 / (16 * 15)
    true = truth[pl.ds(pl.multiple_of(ens * 8, 8), 8), :]
    fields = [seen[m] for m in range(16)]
    slope_sums = [jnp.zeros((8, 128), F32) for _ in range(16)]
    spread = jnp.zeros((8, 128), F32)
    skill = jnp.zeros((8, 128), F32)
    for m in range(16):
        for k in range(m):
            apart = fields[m] - fields[k]
            square = apart * apart + SMOOTH
            tilt = lax.rsqrt(square)
            spread = spread + square * tilt
            tilt = apart * tilt
            slope_sums[m] = slope_sums[m] + tilt
            slope_sums[k] = slope_sums[k] - tilt
    for m in range(16):
        apart = fields[m] - true
        square = apart * apart + SMOOTH
        tilt = lax.rsqrt(square)
        skill = skill + square * tilt
        out[m] = weight * (apart * tilt * (1.0 / 16) - pair_weight * slope_sums[m])
    backs = [
        send(out.at[t[0]], slopes.at[ens], (bsem.at[d], csem.at[d]), t) for d, t in enumerate(ens_others)
    ]
    slopes[ens] = out[ens]
    total = weight * (skill * (1.0 / 16) - pair_weight * spread)
    channel = ens * 8 + lax.broadcasted_iota(jnp.int32, (8, 128), 0)
    loss = jnp.sum(jnp.where(channel < channels, total, 0.0))
    high = loss.astype(BF16).astype(F32)
    rows = lax.broadcasted_iota(jnp.int32, (128, 512), 0)
    lanes = lax.broadcasted_iota(jnp.int32, (128, 512), 1)
    for copy in backs:
        copy.wait_recv()
    slopes_b = slopes[...].reshape(128, 128).astype(BF16)

    def readout_gradient():
        product = dot32(slopes_b, normed_b)
        for h in range(2):
            mine = jnp.where(core == h, 1.0, 0.0)
            part = jnp.where(rows < channels, product[:, 512 * h : 512 * h + 512], 0.0)
            note = jnp.where(lanes == 0, high, jnp.where(lanes == 1, loss - high, 0.0)) * mine
            part = jnp.where(rows == channels, note, part)
            halves[h] = part.astype(BF16).reshape(16, 8, 512)

    readout_gradient()
    pair["half"] = send(halves.at[1 - core], half_in, (pair_s.at[5], pair_r.at[5]), partner)

    d_normed = across(slopes_b, readout[...])
    normed = hidden[...]
    shared = jnp.sum(d_normed * normed, axis=-1, keepdims=True) * (1.0 / 1024)
    d_hidden[...] = (inverse * (d_normed - normed * shared)).astype(BF16)
    for n in range(4):
        cut = slice(256 * n, 256 * n + 256)
        d_attended[:, cut] = columns(d_hidden[...], wm[cut, :]).astype(BF16)

    pair["half"].wait_recv()
    half_sum[...] = (halves[core].astype(F32) + half_in[...].astype(F32)).astype(BF16)
    gather1 = [
        send(half_sum.at[t[0]], g1.at[d], (as1.at[d], ar1.at[d]), t) for d, t in enumerate(ens_others)
    ]

    def by_parity(left, right):
        return (
            jnp.where(early, left, pltpu.roll(right, 64, 1)).astype(BF16),
            jnp.where(early, pltpu.roll(left, 64, 1), right).astype(BF16),
        )

    def join(v):
        return jnp.where(early, v[0:128], v[128:256])

    def retreat(h, carry):
        at = pl.ds(pl.multiple_of(h * 128, 128), 128)
        above = d_attended[:, at]
        soft = probs[h]
        keys2 = apart_heads(keyset[:, at])
        d_probs = columns(above, apart_heads(valueset[:, at]))
        weighted = d_probs * soft
        d_scores = []
        for i in range(2):
            cut = slice(128 * i, 128 * i + 128)
            mean = jnp.sum(weighted[:, cut], axis=-1, keepdims=True)
            d_scores.append(soft[:, cut] * (d_probs[:, cut] - mean) * 0.125)
        d_scores = jnp.concatenate(d_scores, axis=1).astype(BF16)
        d_values = join(across(soft.astype(BF16), above))
        d_keys = join(across(d_scores, queries[:, at]))
        d_queries = dot32(d_scores, keys2)
        parts_ref[0, 0, h], parts_ref[0, 1, h] = by_parity(d_keys, d_values)
        parts_ref[1, 0, h], parts_ref[1, 1, h] = by_parity(d_queries, d_hidden[:, at].astype(F32))
        return carry

    lax.fori_loop(0, 8, retreat, 0)
    for i in range(2):
        pair["part", i] = send(
            parts_ref.at[i, 1 - core], parts_in.at[i], (pair_s.at[3 + i], pair_r.at[3 + i]), partner
        )
    for name in ("grid", "node", "attended", ("part", 0), ("part", 1)):
        pair[name].wait_recv()

    lane = lax.broadcasted_iota(jnp.int32, (1024, 256), 1) % 128

    def products(step, carry):
        mine = [
            jnp.concatenate([parts_ref[i, core, 2 * step + j] for j in range(2)], axis=1) for i in range(2)
        ]
        theirs = [
            jnp.concatenate([parts_in[i, 2 * step + j] for j in range(2)], axis=1) for i in range(2)
        ]
        node = across(acts_ref[0], mine[0]) + across(acts_in[0], theirs[0])
        grid = across(acts_ref[1], mine[1]) + across(acts_in[1], theirs[1])
        mixed = across(acts_ref[2], mine[1]) + across(acts_in[2], theirs[1])
        found = (node.astype(BF16), jnp.where(lane < 64, grid, mixed).astype(BF16))
        for j in range(2):
            column = step * 2 + j
            cz, cx = column // 4, column % 4
            for e in range(16):
                for r in range(2):
                    at_row = e * 64 + r * 32
                    block0 = found[0][at_row : at_row + 32, 128 * j : 128 * j + 128]
                    block1 = found[1][at_row : at_row + 32, 128 * j : 128 * j + 128]
                    work[r, cx, e % 4, cz * 4 + e // 4] = block0
                    work[2 + r, e % 4, cx, cz * 4 + e // 4] = block1
        return carry

    lax.fori_loop(0, 4, products, 0)

    def beside(c, axis, value):
        along_x = (c < 2) == (axis == 0)
        return device(value, y, z, core) if along_x else device(x, value, z, core)

    flips = [(flip1, flip3), (flip3, flip1)] * 2
    places = [(x, y), (x, y), (y, x), (y, x)]
    first, second, third, fourth = {}, {}, {}, {}
    for c in range(4):
        f1, f2 = flips[c]
        p, q = places[c]
        for slot, block in ((1, f2(f1(p))), (0, f1(p))):
            first[c, slot] = send(
                work.at[c, block], r1.at[c, slot], (s1.at[c, slot], q1.at[c, slot]), beside(c, 0, f1(p))
            )
    for c in range(4):
        f1, f2 = flips[c]
        p, q = places[c]
        first[c, 1].wait_recv()
        work[c, f2(p)] = (work[c, f2(p)].astype(F32) + r1[c, 1].astype(F32)).astype(BF16)
        second[c] = send(work.at[c, f2(p)], r2.at[c], (s2.at[c], q2.at[c]), beside(c, 0, f2(p)))

    for copy in gather1:
        copy.wait_recv()
    summed = half_sum[ens].astype(F32)
    for d in range(15):
        summed = summed + g1[d].astype(F32)
    own2[...] = summed.astype(BF16)
    gather2 = [send(own2, g2.at[d], (as2.at[d], ar2.at[d]), t) for d, t in enumerate(space_others)]

    def both(c, p, at):
        return work[c, p, at].astype(F32) + r1[c, 0, at].astype(F32) + r2[c, at].astype(F32)

    for c in range(4):
        f1, f2 = flips[c]
        p, q = places[c]
        first[c, 0].wait_recv()
        second[c].wait_recv()
        for slot, block in ((1, f2(f1(q))), (0, f1(q))):
            work[c, p, block] = both(c, p, block).astype(BF16)
            third[c, slot] = send(
                work.at[c, p, block], r3.at[c, slot], (s3.at[c, slot], q3.at[c, slot]), beside(c, 1, f1(q))
            )

    for copy in gather2:
        copy.wait_recv()
    summed = own2[...].astype(F32)
    for d in range(7):
        summed = summed + g2[d].astype(F32)
    own3[...] = summed.astype(BF16)
    gather3 = [
        send(own3, g3.at[ens], (as3.at[d], ar3.at[d]), t) for d, t in enumerate(ens_others)
    ]
    g3[ens] = own3[...]

    for c in range(4):
        f1, f2 = flips[c]
        p, q = places[c]
        third[c, 1].wait_recv()
        work[c, p, f2(q)] = (both(c, p, f2(q)) + r3[c, 1].astype(F32)).astype(BF16)
        fourth[c] = send(work.at[c, p, f2(q)], r4.at[c], (s4.at[c], q4.at[c]), beside(c, 1, f2(q)))
    for c in range(4):
        p, q = places[c]
        third[c, 0].wait_recv()
        fourth[c].wait_recv()
        block = both(c, p, q) + r3[c, 0].astype(F32) + r4[c].astype(F32)
        block = block.astype(BF16)
        for k in range(8):
            last[k, c] = block[k]
    deep = [
        send(last.at[(z + d + 1) % 8], rz.at[d], (zs.at[d], zr.at[d]), t) for d, t in enumerate(z_others)
    ]

    for copy in gather3:
        copy.wait_recv()
    final = send(g3, g4, (pair_s.at[6], pair_r.at[6]), partner)
    for copy in deep:
        copy.wait_recv()
    grads = last[z].astype(F32)
    for d in range(7):
        grads = grads + rz[d].astype(F32)
    grads_ref[...] = grads
    final.wait_recv()
    for copy in pending:
        copy.wait_send()


def finish_kernel(channels, grads_ref, g3, g4, loss_out, out_out, query_out, key_out, value_out, mix_out):
    core = lax.axis_index("space") % 2
    rows = lax.broadcasted_iota(jnp.int32, (128, 512), 0)
    lanes = lax.broadcasted_iota(jnp.int32, (128, 512), 1)
    here = g3[...].astype(F32).reshape(128, 512)
    there = g4[...].astype(F32).reshape(128, 512)
    low = jnp.where(core == 0, here, there)
    upper = jnp.where(core == 0, there, here)
    out_out[:, 0:512] = low[:channels]
    out_out[:, 512:1024] = upper[:channels]
    notes = jnp.where(lanes < 2, low + upper, 0.0)
    loss_out[0, 0] = jnp.sum(jnp.where(rows == channels, notes, 0.0))
    for r in range(2):
        key_out[32 * r : 32 * r + 32, :] = grads_ref[r][:, 0:64]
        value_out[32 * r : 32 * r + 32, :] = grads_ref[r][:, 64:128]
        query_out[32 * r : 32 * r + 32, :] = grads_ref[2 + r][:, 0:64]
        mix_out[32 * r : 32 * r + 32, :] = grads_ref[2 + r][:, 64:128]


def body(
    grid_hidden, latent, tile_neighbor_index, target, w_query, w_key, w_value, w_mix, readout_weight
):
    channels, points = target.shape
    whole = pl.BlockSpec(memory_space=pltpu.VMEM)
    apart = pl.BlockSpec(memory_space=pl.ANY)
    dma = pltpu.SemaphoreType.DMA
    square = jax.ShapeDtypeStruct((64, 64), F32)

    def vmem(*shape):
        return pltpu.VMEM(shape, BF16)

    half = jax.ShapeDtypeStruct((16, 8, 512), BF16)
    grads, g3, g4 = pl.pallas_call(
        functools.partial(step_kernel, channels, points * lax.axis_size("space")),
        out_shape=(jax.ShapeDtypeStruct((4, 32, 128), F32), half, half),
        in_specs=[apart, apart, whole, whole, apart, apart, apart, apart, whole],
        out_specs=(whole,) * 3,
        scratch_shapes=[vmem(1024, 1024)] * 4
        + [
            vmem(128, 1024), pltpu.VMEM((128, 128), F32), vmem(3, 128, 1024), pltpu.VMEM((8, 128, 256), F32),
            vmem(128, 1024), vmem(128, 1024), vmem(128, 1024), pltpu.VMEM((128, 1024), F32),
            vmem(128, 1024), vmem(128, 1024),
        ]
        + [pltpu.VMEM((16, 8, 128), F32)] * 4
        + [
            vmem(3, 128, 1024),
            vmem(2, 2, 8, 128, 128),
            vmem(3, 128, 1024),
            vmem(2, 8, 128, 128),
            vmem(4, 4, 4, 8, 32, 128),
            vmem(4, 2, 4, 8, 32, 128),
            vmem(4, 4, 8, 32, 128),
            vmem(4, 2, 8, 32, 128),
            vmem(4, 8, 32, 128),
            vmem(8, 4, 32, 128),
            vmem(7, 4, 32, 128),
            vmem(2, 16, 8, 512),
            vmem(16, 8, 512),
            vmem(16, 8, 512),
            vmem(15, 8, 512),
            vmem(8, 512),
            vmem(7, 8, 512),
            vmem(8, 512),
            dma((6,)), dma((2,)), dma((2,)),
            dma((15,)), dma((15,)), dma((15,)), dma((15,)),
            dma((7,)), dma((7,)),
            dma((4, 2)), dma((4, 2)), dma((4,)), dma((4,)),
            dma((4, 2)), dma((4, 2)), dma((4,)), dma((4,)),
            dma((7,)), dma((7,)),
            dma((15,)), dma((15,)), dma((7,)), dma((7,)), dma((15,)), dma((15,)),
        ],
        compiler_params=pltpu.CompilerParams(
            collective_id=1, has_side_effects=True, vmem_limit_bytes=56 << 20
        ),
        name="step",
    )(
        grid_hidden.reshape(points, -1), latent.reshape(points, -1), tile_neighbor_index, target,
        w_query, w_key, w_value, w_mix, readout_weight,
    )
    loss, grad_out, grad_query, grad_key, grad_value, grad_mix = pl.pallas_call(
        functools.partial(finish_kernel, channels),
        out_shape=(
            jax.ShapeDtypeStruct((1, 1), F32),
            jax.ShapeDtypeStruct((channels, 1024), F32),
            square, square, square, square,
        ),
        in_specs=[whole] * 3,
        out_specs=(pl.BlockSpec(memory_space=pltpu.SMEM),) + (whole,) * 5,
        name="finish",
    )(grads, g3, g4)
    return loss.reshape(()), grad_out, grad_query, grad_key, grad_value, grad_mix


def solution(mesh):
    in_specs = (
        P("ens", "space", None),
        P("ens", "space", None),
        P("space", None),
        P(None, "space"),
        P(), P(), P(), P(), P(),
    )
    out_specs = (
        P(), P(),
        P("ens", "space"), P("ens", "space"), P("ens", "space"), P("ens", "space"),
    )
    return jax.shard_map(body, mesh=mesh, in_specs=in_specs, out_specs=out_specs, check_vma=False)
```

time: 124 us -> 91.9 us (0.74); the launches traced: 122 us -> 91.8 us
  matrix products: 24.8 us -> 0 us
  Pallas kernels: 73.8 us -> 91.2 us
  local copies, waits for them, and re-layouts: 13.2 us -> 0 us
  other arithmetic: 6.41 us -> 0 us
  starting transfers between devices: 1.82 us -> 0 us
    dot_general x12 -> x0, matrix products: 23.3 us -> none  [the longest x5 13.4 us: einsum(): return jnp.einsum(spec, a, b, preferred_element_type=F32)]
    pallas_call x2, Pallas kernels: 73.8 us -> 91.2 us  [the longest x1 89.3 us: body(): pl.pallas_call(functools.partial(step_kernel, channels, points * lax.axis...]
    unnamed x39 -> x0, local copies, waits for them, and re-layouts: 4.33 us -> none
    convert_element_type x6 -> x0, local copies, waits for them, and re-layouts: 3.99 us -> none  [the longest x1 1.09 us: body(): attended = attended.reshape(points, features).astype(BF16)]
    another operation x3 -> x0, other arithmetic: 2.43 us -> none  [the longest x1 1.3 us: body(): jnp.stack([by_parity(d_keys, d_values), by_parity(d_queries, by_heads(d_h...]
    another operation x3 -> x0, local copies, waits for them, and re-layouts: 2.06 us -> none  [the longest x2 2.02 us: body(): jnp.stack([by_parity(d_keys, d_values), by_parity(d_queries, by_heads(d_h...]
    ppermute x2 -> x0, starting transfers between devices: 1.82 us -> none  [the longest x1 1.73 us: with_halo(): after = lax.ppermute(leading, axis, down)]
    sub x1 -> x0, matrix products: 1.49 us -> none  [body(): raised = jnp.exp(scores - jnp.max(scores, axis=-1, keepdims=True))]
  transfers between devices with their start and end apart: 2 -> 0, of which waited for: 1 -> 0; matrix products, arithmetic and copies ran while one was open for 4% -> 0% of each run, Pallas kernels for 0% -> 0%
where the time goes in v2:
time: 91.9 us; the launch traced here: 91.8 us
  Pallas kernels  91.2 us (99%)
    pallas_call x1, Pallas kernels, body(): pl.pallas_call(functools.partial(step_kernel, channels, points * lax.axis...  89.3 us
    pallas_call x1, Pallas kernels, body(): pl.pallas_call(functools.partial(finish_kernel, channels), out_shape=(jax...  1.88 us

profile of v2, /device:TPU:6, one launch (start us, length us, event | category | flops | bytes accessed | tf_op | source)
XLA Modules:
  0.0 91.8 jit_solution(9753757715044155948)
XLA Ops:
  0.6 89.3 %step.1 = (f32[4,32,128]{2,1,0:T(8,128)}, bf16[16,8,512]{2,1,0:T(8,128)(2,1)}, bf16[16,8,512]{2,1,0:T(8,128)(2,1)}) custom-call(bf16[128,1024]{1,0:T(8,128)(2,1)} %bitcast.3, bf16[128,1024]{1,0:T(8,128)(2,1)} %bitcast.4, s32[1,128]{1,0:T(1,128)} %index_ref.1, f32[100,128]{1,0:T(8,128)} %target_ref.1, bf16[1024,1024]{1,0:T(8,128)(2,1)} %wq_ref.1, ...), custom_call_target="tpu_custom_call" | custom-call | tf_op jit(solution)/shard_map/step/pallas_call | solution.py:423
  89.9 1.9 %finish.1 = (f32[1,1]{1,0:T(1,128)}, f32[100,1024]{1,0:T(8,128)}, f32[64,64]{1,0:T(8,128)}, f32[64,64]{1,0:T(8,128)}, f32[64,64]{1,0:T(8,128)}, /*index=5*/f32[64,64]{1,0:T(8,128)}) custom-call(f32[4,32,128]{2,1,0:T(8,128)} %get-tuple-element.15.grads_ref, bf16[16,8,512]{2,1,0:T(8,128)(2,1)} %get-tuple-element.16.g3, bf16[16,8,512]{2,1,0:T(8,128)(2,1)} %get-tuple-element.17.g4), custom_call_target="tpu_custom_call" | custom-call | tf_op jit(solution)/shard_map/finish/pallas_call | solution.py:470

commit v3 on v2

--- a/solution.py
+++ b/solution.py
@@ -70,11 +70,11 @@
     grads_ref, g3, g4,
     wq, wk, wv, wm, readout, truth, near, probs, queries, keyset, valueset, hidden, d_hidden, d_attended,
     field, seen, out, slopes,
-    acts_ref, parts_ref,
-    acts_in, parts_in, work, r1, r2, r3, r4, last, rz,
+    acts_ref, parts_ref, parts_in, nodes, grids, mixes,
+    work, r3, r4, last, rz,
     halves, half_in, half_sum, g1, own2, g2, own3,
     local, halo_s, halo_r, ssem, rsem, bsem, csem,
-    pair_s, pair_r, s1, q1, s2, q2, s3, q3, s4, q4, zs, zr,
+    pair_s, pair_r, gs, gr, ps, pr, s3, q3, s4, q4, zs, zr,
     as1, ar1, as2, ar2, as3, ar3,
 ):
     x, y, z, core = coordinates()
@@ -89,10 +89,19 @@
     after = (ens, (space + 1) % 16)
     before = (ens, (space + 15) % 16)
     outside = (ens, (space + 16 + 2 * core - 1) % 16)
-    targets = [partner, outside] + ens_others + space_others + z_only
+    along_x = [device((x + d) % 4, y, z, 1 - core) for d in range(1, 4)]
+    along_y = [device(x, (y + d) % 4, z, 1 - core) for d in range(1, 4)]
+    mirrored = [device(y, x, (z + d) % 8, core) for d in range(8)]
+    targets = [partner, outside] + ens_others + space_others + z_only + along_x + along_y
     barrier = pltpu.get_barrier_semaphore()
     for target in targets:
         pl.semaphore_signal(barrier, inc=1, device_id=target, device_id_type=MESH)
+
+    @pl.when(x != y)
+    def _():
+        for target in mirrored:
+            pl.semaphore_signal(barrier, inc=1, device_id=target, device_id_type=MESH)
+
 
     loads = []
     pairs_of = (
@@ -106,9 +115,19 @@
     readout[0:channels, :] = readout_ref[...]
     truth[96:128, :] = jnp.zeros((32, 128), F32)
     truth[0:channels, :] = target_ref[...]
+    def turned(dst, source):
+        for n in range(8):
+            dst[128 * n : 128 * n + 128, :] = source[:, 128 * n : 128 * n + 128].T
+
     loads[0].wait()
+    turned(grids.at[y, core], acts_ref[1])
+    loads[2].wait()
+    wide_dot(acts_ref[1], wq, queries)
+    place = (index_ref[...] - (space - 1) * 128 + 2048) & 2047
+    node_id = lax.broadcasted_iota(jnp.int32, (384, 128), 0)
+    chosen = jnp.where(node_id == place, 1.0, 0.0).astype(BF16)
     loads[1].wait()
-    pl.semaphore_wait(barrier, len(targets))
+    pl.semaphore_wait(barrier, len(targets) + jnp.where(x != y, 8, 0))
 
     pending = []
 
@@ -118,29 +137,63 @@
         pending.append(copy)
         return copy
 
+    def on_x(p, c):
+        return device(p, y, z, c)
+
+    def on_y(p, c):
+        return device(x, p, z, c)
+
+    tiles = ((nodes, x, on_x), (grids, y, on_y), (mixes, y, on_y))
+    ring = {}
+
+    def move(i, k, ref, target):
+        ring[i, k] = send(ref, ref, (gs.at[i, k], gr.at[i, k]), target)
+
+    def spread_tile(i):
+        buf, p, beside = tiles[i]
+        move(i, 0, buf.at[p, core], beside((p + 1) % 4, core))
+        move(i, 1, buf.at[p, core], beside((p + 3) % 4, core))
+        move(i, 2, buf.at[p, core], partner)
+
+    def forward_tile(i):
+        buf, p, beside = tiles[i]
+        above, below = (p + 1) % 4, (p + 3) % 4
+        ring[i, 0].wait_recv()
+        ring[i, 1].wait_recv()
+        move(i, 3, buf.at[below, core, 0:512], beside(above, core))
+        move(i, 4, buf.at[above, core, 512:1024], beside(below, core))
+        move(i, 5, buf.at[below, core], partner)
+        move(i, 6, buf.at[above, core], partner)
+
+    def close_tile(i):
+        buf, p, beside = tiles[i]
+        ring[i, 3].wait_recv()
+        ring[i, 4].wait_recv()
+        move(i, 7, buf.at[(p + 2) % 4, core], partner)
+
+    def have_tile(i):
+        for k in (2, 5, 6, 7):
+            ring[i, k].wait_recv()
+
     halo = [
         send(near.at[1], near.at[0], (halo_s.at[0], halo_r.at[0]), after),
         send(near.at[1], near.at[2], (halo_s.at[1], halo_r.at[1]), before),
     ]
     pair = {}
-    pair["grid"] = send(acts_ref.at[1], acts_in.at[1], (pair_s.at[1], pair_r.at[1]), partner)
-    loads[2].wait()
-    wide_dot(acts_ref[1], wq, queries)
-    place = (index_ref[...] - (space - 1) * 128 + 2048) & 2047
-    node_id = lax.broadcasted_iota(jnp.int32, (384, 128), 0)
-    chosen = jnp.where(node_id == place, 1.0, 0.0).astype(BF16)
+    pair = {}
+    spread_tile(1)
     for copy in halo:
         copy.wait_recv()
     for n in range(4):
         cut = slice(256 * n, 256 * n + 256)
         found = sum(across(chosen[128 * i : 128 * i + 128], near[i, :, cut]) for i in range(3))
         acts_ref[0, :, cut] = found.astype(BF16)
-    pair["node"] = send(acts_ref.at[0], acts_in.at[0], (pair_s.at[0], pair_r.at[0]), partner)
     loads[3].wait()
     wide_dot(acts_ref[0], wk, keyset)
     loads[4].wait()
     wide_dot(acts_ref[0], wv, valueset)
 
+    forward_tile(1)
     early = lax.broadcasted_iota(jnp.int32, (128, 128), 1) < 64
 
     def apart_heads(v):
@@ -161,7 +214,6 @@
         return carry
 
     lax.fori_loop(0, 8, attend, 0)
-    pair["attended"] = send(acts_ref.at[2], acts_in.at[2], (pair_s.at[2], pair_r.at[2]), partner)
     loads[5].wait()
     wide_dot(acts_ref[2], wm, hidden)
     full = hidden[...] + acts_ref[1].astype(F32)
@@ -174,6 +226,8 @@
         send(field.at[t[0]], seen.at[ens], (ssem.at[d], rsem.at[d]), t) for d, t in enumerate(ens_others)
     ]
     seen[ens] = field[ens]
+    turned(nodes.at[x, core], acts_ref[0])
+    spread_tile(0)
     for copy in sends:
         copy.wait_recv()
     weight = (channels * points_all) ** (-0.5)
@@ -202,6 +256,9 @@
         send(out.at[t[0]], slopes.at[ens], (bsem.at[d], csem.at[d]), t) for d, t in enumerate(ens_others)
     ]
     slopes[ens] = out[ens]
+    turned(mixes.at[y, core], acts_ref[2])
+    spread_tile(2)
+    close_tile(1)
     total = weight * (skill * (1.0 / 16) - pair_weight * spread)
     channel = ens * 8 + lax.broadcasted_iota(jnp.int32, (8, 128), 0)
     loss = jnp.sum(jnp.where(channel < channels, total, 0.0))
@@ -232,6 +289,8 @@
         cut = slice(256 * n, 256 * n + 256)
         d_attended[:, cut] = columns(d_hidden[...], wm[cut, :]).astype(BF16)
 
+    forward_tile(0)
+    forward_tile(2)
     pair["half"].wait_recv()
     half_sum[...] = (halves[core].astype(F32) + half_in[...].astype(F32)).astype(BF16)
     gather1 = [
@@ -263,65 +322,75 @@
         d_values = join(across(soft.astype(BF16), above))
         d_keys = join(across(d_scores, queries[:, at]))
         d_queries = dot32(d_scores, keys2)
-        parts_ref[0, 0, h], parts_ref[0, 1, h] = by_parity(d_keys, d_values)
-        parts_ref[1, 0, h], parts_ref[1, 1, h] = by_parity(d_queries, d_hidden[:, at].astype(F32))
+        side = pl.ds(pl.multiple_of((h // 4) * 128, 128), 128)
+        for i, (left, right) in enumerate(((d_keys, d_values), (d_queries, d_hidden[:, at].astype(F32)))):
+            for parity, block in enumerate(by_parity(left, right)):
+                parts_ref[i, parity, h % 4, :, side] = block
         return carry
 
     lax.fori_loop(0, 8, retreat, 0)
-    for i in range(2):
-        pair["part", i] = send(
-            parts_ref.at[i, 1 - core], parts_in.at[i], (pair_s.at[3 + i], pair_r.at[3 + i]), partner
-        )
-    for name in ("grid", "node", "attended", ("part", 0), ("part", 1)):
-        pair[name].wait_recv()
-
-    lane = lax.broadcasted_iota(jnp.int32, (1024, 256), 1) % 128
-
-    def products(step, carry):
-        mine = [
-            jnp.concatenate([parts_ref[i, core, 2 * step + j] for j in range(2)], axis=1) for i in range(2)
-        ]
-        theirs = [
-            jnp.concatenate([parts_in[i, 2 * step + j] for j in range(2)], axis=1) for i in range(2)
-        ]
-        node = across(acts_ref[0], mine[0]) + across(acts_in[0], theirs[0])
-        grid = across(acts_ref[1], mine[1]) + across(acts_in[1], theirs[1])
-        mixed = across(acts_ref[2], mine[1]) + across(acts_in[2], theirs[1])
-        found = (node.astype(BF16), jnp.where(lane < 64, grid, mixed).astype(BF16))
-        for j in range(2):
-            column = step * 2 + j
-            cz, cx = column // 4, column % 4
-            for e in range(16):
-                for r in range(2):
-                    at_row = e * 64 + r * 32
-                    block0 = found[0][at_row : at_row + 32, 128 * j : 128 * j + 128]
-                    block1 = found[1][at_row : at_row + 32, 128 * j : 128 * j + 128]
-                    work[r, cx, e % 4, cz * 4 + e // 4] = block0
-                    work[2 + r, e % 4, cx, cz * 4 + e // 4] = block1
+    parts = {}
+    for i, (p, beside) in enumerate(((x, on_x), (y, on_y))):
+        for k in range(1, 8):
+            to, c = (p + k // 2) % 4, (core + k) % 2
+            parts[i, k] = send(
+                parts_ref.at[i, c, to], parts_in.at[i, p, core], (ps.at[i, k], pr.at[i, k]), beside(to, c)
+            )
+        parts_in[i, p, core] = parts_ref[i, core, p]
+    close_tile(0)
+    close_tile(2)
+
+    lane = lax.broadcasted_iota(jnp.int32, (256, 256), 1) % 128
+
+    def store(base, step, block):
+        block = block.astype(BF16)
+        for w in range(4):
+            for r in range(2):
+                for h in range(2):
+                    row = w * 64 + r * 32
+                    work[base + r, w, h * 4 + step] = block[row : row + 32, 128 * h : 128 * h + 128]
+
+    def product(buf, i, step):
+        at = pl.ds(pl.multiple_of(step * 256, 256), 256)
+        total = jnp.zeros((256, 256), F32)
+        for t in range(4):
+            left = jnp.concatenate([buf[t, 0, at, :], buf[t, 1, at, :]], axis=1)
+            total = total + dot32(left, parts_in[i, t].reshape(256, 256))
+        return total
+
+    def first_product(step, carry):
+        store(0, step, product(nodes, 0, step))
         return carry
 
-    lax.fori_loop(0, 4, products, 0)
-
-    def beside(c, axis, value):
-        along_x = (c < 2) == (axis == 0)
-        return device(value, y, z, core) if along_x else device(x, value, z, core)
+    def second_product(step, carry):
+        store(2, step, jnp.where(lane < 64, product(grids, 1, step), product(mixes, 1, step)))
+        return carry
 
     flips = [(flip1, flip3), (flip3, flip1)] * 2
-    places = [(x, y), (x, y), (y, x), (y, x)]
-    first, second, third, fourth = {}, {}, {}, {}
-    for c in range(4):
+    places = [(y, on_y), (y, on_y), (x, on_x), (x, on_x)]
+    third, fourth = {}, {}
+
+    def halve(c):
         f1, f2 = flips[c]
-        p, q = places[c]
-        for slot, block in ((1, f2(f1(p))), (0, f1(p))):
-            first[c, slot] = send(
-                work.at[c, block], r1.at[c, slot], (s1.at[c, slot], q1.at[c, slot]), beside(c, 0, f1(p))
+        q, beside = places[c]
+        for slot, block in ((1, f2(f1(q))), (0, f1(q))):
+            third[c, slot] = send(
+                work.at[c, block], r3.at[c, slot], (s3.at[c, slot], q3.at[c, slot]), beside(f1(q), core)
             )
-    for c in range(4):
-        f1, f2 = flips[c]
-        p, q = places[c]
-        first[c, 1].wait_recv()
-        work[c, f2(p)] = (work[c, f2(p)].astype(F32) + r1[c, 1].astype(F32)).astype(BF16)
-        second[c] = send(work.at[c, f2(p)], r2.at[c], (s2.at[c], q2.at[c]), beside(c, 0, f2(p)))
+
+    for k in range(1, 8):
+        parts[0, k].wait_recv()
+    have_tile(0)
+    lax.fori_loop(0, 4, first_product, 0)
+    halve(0)
+    halve(1)
+    for k in range(1, 8):
+        parts[1, k].wait_recv()
+    have_tile(1)
+    have_tile(2)
+    lax.fori_loop(0, 4, second_product, 0)
+    halve(2)
+    halve(3)
 
     for copy in gather1:
         copy.wait_recv()
@@ -330,20 +399,6 @@
         summed = summed + g1[d].astype(F32)
     own2[...] = summed.astype(BF16)
     gather2 = [send(own2, g2.at[d], (as2.at[d], ar2.at[d]), t) for d, t in enumerate(space_others)]
-
-    def both(c, p, at):
-        return work[c, p, at].astype(F32) + r1[c, 0, at].astype(F32) + r2[c, at].astype(F32)
-
-    for c in range(4):
-        f1, f2 = flips[c]
-        p, q = places[c]
-        first[c, 0].wait_recv()
-        second[c].wait_recv()
-        for slot, block in ((1, f2(f1(q))), (0, f1(q))):
-            work[c, p, block] = both(c, p, block).astype(BF16)
-            third[c, slot] = send(
-                work.at[c, p, block], r3.at[c, slot], (s3.at[c, slot], q3.at[c, slot]), beside(c, 1, f1(q))
-            )
 
     for copy in gather2:
         copy.wait_recv()
@@ -358,31 +413,48 @@
 
     for c in range(4):
         f1, f2 = flips[c]
-        p, q = places[c]
+        q, beside = places[c]
         third[c, 1].wait_recv()
-        work[c, p, f2(q)] = (both(c, p, f2(q)) + r3[c, 1].astype(F32)).astype(BF16)
-        fourth[c] = send(work.at[c, p, f2(q)], r4.at[c], (s4.at[c], q4.at[c]), beside(c, 1, f2(q)))
-    for c in range(4):
-        p, q = places[c]
-        third[c, 0].wait_recv()
-        fourth[c].wait_recv()
-        block = both(c, p, q) + r3[c, 0].astype(F32) + r4[c].astype(F32)
-        block = block.astype(BF16)
-        for k in range(8):
-            last[k, c] = block[k]
-    deep = [
-        send(last.at[(z + d + 1) % 8], rz.at[d], (zs.at[d], zr.at[d]), t) for d, t in enumerate(z_others)
-    ]
+        work[c, f2(q)] = (work[c, f2(q)].astype(F32) + r3[c, 1].astype(F32)).astype(BF16)
+        fourth[c] = send(work.at[c, f2(q)], r4.at[c], (s4.at[c], q4.at[c]), beside(f2(q), core))
+    deep = []
+    for i in range(2):
+        for c in (2 * i, 2 * i + 1):
+            q = places[c][0]
+            third[c, 0].wait_recv()
+            fourth[c].wait_recv()
+            block = work[c, q].astype(F32) + r3[c, 0].astype(F32) + r4[c].astype(F32)
+            block = block.astype(BF16)
+            for k in range(8):
+                last[i, k, c % 2] = block[k]
+        for d in range(1, 8):
+            target = z_others[d - 1] if i == 0 else mirrored[d]
+            deep.append(send(last.at[i, (z + d) % 8], rz.at[i, d], (zs.at[i, d], zr.at[i, d]), target))
+    mirror = remote(last.at[1, z], rz.at[1, 0], (zs.at[1, 0], zr.at[1, 0]), mirrored[0])
+
+    @pl.when(x != y)
+    def _():
+        mirror.start()
+
+    @pl.when(x == y)
+    def _():
+        rz[1, 0] = last[1, z]
 
     for copy in gather3:
         copy.wait_recv()
     final = send(g3, g4, (pair_s.at[6], pair_r.at[6]), partner)
     for copy in deep:
         copy.wait_recv()
-    grads = last[z].astype(F32)
-    for d in range(7):
-        grads = grads + rz[d].astype(F32)
-    grads_ref[...] = grads
+
+    @pl.when(x != y)
+    def _():
+        mirror.wait()
+
+    for i in range(2):
+        grads = (last[0, z] if i == 0 else rz[1, 0]).astype(F32)
+        for d in range(1, 8):
+            grads = grads + rz[i, d].astype(F32)
+        grads_ref[2 * i : 2 * i + 2] = grads
     final.wait_recv()
     for copy in pending:
         copy.wait_send()
@@ -434,16 +506,16 @@
         + [pltpu.VMEM((16, 8, 128), F32)] * 4
         + [
             vmem(3, 128, 1024),
-            vmem(2, 2, 8, 128, 128),
-            vmem(3, 128, 1024),
-            vmem(2, 8, 128, 128),
-            vmem(4, 4, 4, 8, 32, 128),
-            vmem(4, 2, 4, 8, 32, 128),
+            vmem(2, 2, 4, 128, 256),
+            vmem(2, 4, 2, 128, 256),
+            vmem(4, 2, 1024, 128),
+            vmem(4, 2, 1024, 128),
+            vmem(4, 2, 1024, 128),
             vmem(4, 4, 8, 32, 128),
             vmem(4, 2, 8, 32, 128),
             vmem(4, 8, 32, 128),
-            vmem(8, 4, 32, 128),
-            vmem(7, 4, 32, 128),
+            vmem(2, 8, 2, 32, 128),
+            vmem(2, 8, 2, 32, 128),
             vmem(2, 16, 8, 512),
             vmem(16, 8, 512),
             vmem(16, 8, 512),
@@ -453,10 +525,8 @@
             vmem(8, 512),
             dma((6,)), dma((2,)), dma((2,)),
             dma((15,)), dma((15,)), dma((15,)), dma((15,)),
-            dma((7,)), dma((7,)),
-            dma((4, 2)), dma((4, 2)), dma((4,)), dma((4,)),
-            dma((4, 2)), dma((4, 2)), dma((4,)), dma((4,)),
-            dma((7,)), dma((7,)),
+            dma((7,)), dma((7,)), dma((3, 8)), dma((3, 8)), dma((2, 8)), dma((2, 8)),
+            dma((4, 2)), dma((4, 2)), dma((4,)), dma((4,)), dma((2, 8)), dma((2, 8)),
             dma((15,)), dma((15,)), dma((7,)), dma((7,)), dma((15,)), dma((15,)),
         ],
         compiler_params=pltpu.CompilerParams(

time: 91.9 us -> 84.4 us (0.918)
  Pallas kernels: 91.2 us -> 83.6 us
    pallas_call x1, Pallas kernels: 89.3 us -> 81.8 us  [body(): pl.pallas_call(functools.partial(step_kernel, channels, points * lax.axis...]
where the time goes in v3:
time: 84.4 us; the launch traced here: 84.3 us
  Pallas kernels  83.6 us (99%)
    pallas_call x1, Pallas kernels, body(): pl.pallas_call(functools.partial(step_kernel, channels, points * lax.axis...  81.8 us
    pallas_call x1, Pallas kernels, body(): pl.pallas_call(functools.partial(finish_kernel, channels), out_shape=(jax...  1.88 us

profile of v3, /device:TPU:6, one launch (start us, length us, event | category | flops | bytes accessed | tf_op | source)
XLA Modules:
  0.0 84.3 jit_solution(7930328949368043064)
XLA Ops:
  0.6 81.8 %step.1 = (f32[4,32,128]{2,1,0:T(8,128)}, bf16[16,8,512]{2,1,0:T(8,128)(2,1)}, bf16[16,8,512]{2,1,0:T(8,128)(2,1)}) custom-call(bf16[128,1024]{1,0:T(8,128)(2,1)} %bitcast.3, bf16[128,1024]{1,0:T(8,128)(2,1)} %bitcast.4, s32[1,128]{1,0:T(1,128)} %index_ref.1, f32[100,128]{1,0:T(8,128)} %target_ref.1, bf16[1024,1024]{1,0:T(8,128)(2,1)} %wq_ref.1, ...), custom_call_target="tpu_custom_call" | custom-call | tf_op jit(solution)/shard_map/step/pallas_call | solution.py:495
  82.4 1.9 %finish.1 = (f32[1,1]{1,0:T(1,128)}, f32[100,1024]{1,0:T(8,128)}, f32[64,64]{1,0:T(8,128)}, f32[64,64]{1,0:T(8,128)}, f32[64,64]{1,0:T(8,128)}, /*index=5*/f32[64,64]{1,0:T(8,128)}) custom-call(f32[4,32,128]{2,1,0:T(8,128)} %get-tuple-element.15.grads_ref, bf16[16,8,512]{2,1,0:T(8,128)(2,1)} %get-tuple-element.16.g3, bf16[16,8,512]{2,1,0:T(8,128)(2,1)} %get-tuple-element.17.g4), custom_call_target="tpu_custom_call" | custom-call | tf_op jit(solution)/shard_map/finish/pallas_call | solution.py:540

commit v4 on v3

--- a/solution.py
+++ b/solution.py
@@ -70,7 +70,7 @@
     grads_ref, g3, g4,
     wq, wk, wv, wm, readout, truth, near, probs, queries, keyset, valueset, hidden, d_hidden, d_attended,
     field, seen, out, slopes,
-    acts_ref, parts_ref, parts_in, nodes, grids, mixes,
+    acts_ref, kv_out, q_out, m_out, kv_in, q_in, m_in, mixed, nodes, grids, mixes,
     work, r3, r4, last, rz,
     halves, half_in, half_sum, g1, own2, g2, own3,
     local, halo_s, halo_r, ssem, rsem, bsem, csem,
@@ -213,7 +213,7 @@
         acts_ref[2, :, at] = dot32(soft.astype(BF16), apart_heads(valueset[:, at])).astype(BF16)
         return carry
 
-    lax.fori_loop(0, 8, attend, 0)
+    lax.fori_loop(0, 8, attend, 0, unroll=2)
     loads[5].wait()
     wide_dot(acts_ref[2], wm, hidden)
     full = hidden[...] + acts_ref[1].astype(F32)
@@ -278,39 +278,44 @@
             part = jnp.where(rows == channels, note, part)
             halves[h] = part.astype(BF16).reshape(16, 8, 512)
 
-    readout_gradient()
-    pair["half"] = send(halves.at[1 - core], half_in, (pair_s.at[5], pair_r.at[5]), partner)
+    def by_parity(left, right):
+        near_half = lax.broadcasted_iota(jnp.int32, left.shape, 1) < 64
+        return (
+            jnp.where(near_half, left, pltpu.roll(right, 64, 1)).astype(BF16),
+            jnp.where(near_half, pltpu.roll(left, 64, 1), right).astype(BF16),
+        )
+
+    parts = {}
+
+    def exchange(i, k, src, dst, ring_of):
+        p, beside = ring_of
+        to, c = (p + k // 2) % 4, (core + k) % 2
+        parts[i, k] = send(src.at[c, to], dst.at[p, core], (ps.at[i, k], pr.at[i, k]), beside(to, c))
 
     d_normed = across(slopes_b, readout[...])
     normed = hidden[...]
     shared = jnp.sum(d_normed * normed, axis=-1, keepdims=True) * (1.0 / 1024)
     d_hidden[...] = (inverse * (d_normed - normed * shared)).astype(BF16)
     for n in range(4):
+        left = d_hidden[:, 128 * n : 128 * n + 128].astype(F32)
+        right = d_hidden[:, 128 * n + 512 : 128 * n + 640].astype(F32)
+        m_out[0, n], m_out[1, n] = by_parity(left, right)
+    for k in (4, 5, 2, 3, 6, 7, 1):
+        exchange(2, k, m_out, m_in, (y, on_y))
+    m_in[y, core] = m_out[core, y]
+    for n in range(4):
         cut = slice(256 * n, 256 * n + 256)
         d_attended[:, cut] = columns(d_hidden[...], wm[cut, :]).astype(BF16)
 
     forward_tile(0)
     forward_tile(2)
-    pair["half"].wait_recv()
-    half_sum[...] = (halves[core].astype(F32) + half_in[...].astype(F32)).astype(BF16)
-    gather1 = [
-        send(half_sum.at[t[0]], g1.at[d], (as1.at[d], ar1.at[d]), t) for d, t in enumerate(ens_others)
-    ]
-
-    def by_parity(left, right):
-        return (
-            jnp.where(early, left, pltpu.roll(right, 64, 1)).astype(BF16),
-            jnp.where(early, pltpu.roll(left, 64, 1), right).astype(BF16),
-        )
-
     def join(v):
         return jnp.where(early, v[0:128], v[128:256])
 
-    def retreat(h, carry):
+    def retreat(h):
         at = pl.ds(pl.multiple_of(h * 128, 128), 128)
         above = d_attended[:, at]
         soft = probs[h]
-        keys2 = apart_heads(keyset[:, at])
         d_probs = columns(above, apart_heads(valueset[:, at]))
         weighted = d_probs * soft
         d_scores = []
@@ -321,49 +326,65 @@
         d_scores = jnp.concatenate(d_scores, axis=1).astype(BF16)
         d_values = join(across(soft.astype(BF16), above))
         d_keys = join(across(d_scores, queries[:, at]))
-        d_queries = dot32(d_scores, keys2)
-        side = pl.ds(pl.multiple_of((h // 4) * 128, 128), 128)
-        for i, (left, right) in enumerate(((d_keys, d_values), (d_queries, d_hidden[:, at].astype(F32)))):
-            for parity, block in enumerate(by_parity(left, right)):
-                parts_ref[i, parity, h % 4, :, side] = block
-        return carry
-
-    lax.fori_loop(0, 8, retreat, 0)
-    parts = {}
-    for i, (p, beside) in enumerate(((x, on_x), (y, on_y))):
-        for k in range(1, 8):
-            to, c = (p + k // 2) % 4, (core + k) % 2
-            parts[i, k] = send(
-                parts_ref.at[i, c, to], parts_in.at[i, p, core], (ps.at[i, k], pr.at[i, k]), beside(to, c)
-            )
-        parts_in[i, p, core] = parts_ref[i, core, p]
+        d_queries = dot32(d_scores, apart_heads(keyset[:, at]))
+        return d_keys, d_values, d_queries
+
+    for d in (2, 1, 3, 0):
+        to = (x + d) % 4
+        kinds = list(zip(retreat(to), retreat(to + 4)))
+        for i in range(2):
+            kv_out[0, to, i], kv_out[1, to, i] = by_parity(*kinds[i])
+        q_out[0, to], q_out[1, to] = by_parity(*kinds[2])
+        for k in (2 * d, 2 * d + 1):
+            if k:
+                exchange(0, k, kv_out, kv_in, (x, on_x))
+    for k in (4, 5, 2, 3, 6, 7, 1):
+        exchange(1, k, q_out, q_in, (y, on_y))
+    kv_in[x, core] = kv_out[core, x]
+    q_in[y, core] = q_out[core, y]
     close_tile(0)
     close_tile(2)
-
-    lane = lax.broadcasted_iota(jnp.int32, (256, 256), 1) % 128
-
-    def store(base, step, block):
-        block = block.astype(BF16)
-        for w in range(4):
-            for r in range(2):
-                for h in range(2):
+    readout_gradient()
+    pair["half"] = send(halves.at[1 - core], half_in, (pair_s.at[5], pair_r.at[5]), partner)
+
+    pair["half"].wait_recv()
+    half_sum[...] = (halves[core].astype(F32) + half_in[...].astype(F32)).astype(BF16)
+    gather1 = [
+        send(half_sum.at[t[0]], g1.at[d], (as1.at[d], ar1.at[d]), t) for d, t in enumerate(ens_others)
+    ]
+
+
+    def store(base, step, left, right):
+        for h, block in enumerate(by_parity(left, right)):
+            for w in range(4):
+                for r in range(2):
                     row = w * 64 + r * 32
-                    work[base + r, w, h * 4 + step] = block[row : row + 32, 128 * h : 128 * h + 128]
-
-    def product(buf, i, step):
-        at = pl.ds(pl.multiple_of(step * 256, 256), 256)
-        total = jnp.zeros((256, 256), F32)
+                    work[base + r, w, h * 4 + step] = block[row : row + 32]
+
+    def product(buf, at, right):
+        total = None
         for t in range(4):
             left = jnp.concatenate([buf[t, 0, at, :], buf[t, 1, at, :]], axis=1)
-            total = total + dot32(left, parts_in[i, t].reshape(256, 256))
+            term = dot32(left, right(t))
+            total = term if total is None else total + term
         return total
 
+    def keys_values(t):
+        return jnp.concatenate([kv_in[t, :, i].reshape(256, 128) for i in range(2)], axis=1)
+
     def first_product(step, carry):
-        store(0, step, product(nodes, 0, step))
+        found = product(nodes, pl.ds(pl.multiple_of(step * 256, 256), 256), keys_values)
+        store(0, step, found[:, 0:128], found[:, 128:256])
         return carry
 
+    def mix_product(step, carry):
+        at = pl.ds(pl.multiple_of(step * 256, 256), 256)
+        mixed[at, :] = product(mixes, at, lambda t: m_in[t].reshape(256, 128))
+        return carry
+
     def second_product(step, carry):
-        store(2, step, jnp.where(lane < 64, product(grids, 1, step), product(mixes, 1, step)))
+        at = pl.ds(pl.multiple_of(step * 256, 256), 256)
+        store(2, step, product(grids, at, lambda t: q_in[t].reshape(256, 128)), mixed[at, :])
         return carry
 
     flips = [(flip1, flip3), (flip3, flip1)] * 2
@@ -385,12 +406,9 @@
     halve(0)
     halve(1)
     for k in range(1, 8):
-        parts[1, k].wait_recv()
-    have_tile(1)
+        parts[2, k].wait_recv()
     have_tile(2)
-    lax.fori_loop(0, 4, second_product, 0)
-    halve(2)
-    halve(3)
+    lax.fori_loop(0, 4, mix_product, 0)
 
     for copy in gather1:
         copy.wait_recv()
@@ -400,6 +418,19 @@
     own2[...] = summed.astype(BF16)
     gather2 = [send(own2, g2.at[d], (as2.at[d], ar2.at[d]), t) for d, t in enumerate(space_others)]
 
+    for k in range(1, 8):
+        parts[1, k].wait_recv()
+    have_tile(1)
+    lax.fori_loop(0, 4, second_product, 0)
+    halve(2)
+    halve(3)
+
+    for c in range(4):
+        f1, f2 = flips[c]
+        q, beside = places[c]
+        third[c, 1].wait_recv()
+        work[c, f2(q)] = (work[c, f2(q)].astype(F32) + r3[c, 1].astype(F32)).astype(BF16)
+        fourth[c] = send(work.at[c, f2(q)], r4.at[c], (s4.at[c], q4.at[c]), beside(f2(q), core))
     for copy in gather2:
         copy.wait_recv()
     summed = own2[...].astype(F32)
@@ -411,12 +442,6 @@
     ]
     g3[ens] = own3[...]
 
-    for c in range(4):
-        f1, f2 = flips[c]
-        q, beside = places[c]
-        third[c, 1].wait_recv()
-        work[c, f2(q)] = (work[c, f2(q)].astype(F32) + r3[c, 1].astype(F32)).astype(BF16)
-        fourth[c] = send(work.at[c, f2(q)], r4.at[c], (s4.at[c], q4.at[c]), beside(f2(q), core))
     deep = []
     for i in range(2):
         for c in (2 * i, 2 * i + 1):
@@ -506,8 +531,13 @@
         + [pltpu.VMEM((16, 8, 128), F32)] * 4
         + [
             vmem(3, 128, 1024),
-            vmem(2, 2, 4, 128, 256),
-            vmem(2, 4, 2, 128, 256),
+            vmem(2, 4, 2, 128, 128),
+            vmem(2, 4, 128, 128),
+            vmem(2, 4, 128, 128),
+            vmem(4, 2, 2, 128, 128),
+            vmem(4, 2, 128, 128),
+            vmem(4, 2, 128, 128),
+            pltpu.VMEM((1024, 128), F32),
             vmem(4, 2, 1024, 128),
             vmem(4, 2, 1024, 128),
             vmem(4, 2, 1024, 128),
@@ -525,7 +555,7 @@
             vmem(8, 512),
             dma((6,)), dma((2,)), dma((2,)),
             dma((15,)), dma((15,)), dma((15,)), dma((15,)),
-            dma((7,)), dma((7,)), dma((3, 8)), dma((3, 8)), dma((2, 8)), dma((2, 8)),
+            dma((7,)), dma((7,)), dma((3, 8)), dma((3, 8)), dma((3, 8)), dma((3, 8)),
             dma((4, 2)), dma((4, 2)), dma((4,)), dma((4,)), dma((2, 8)), dma((2, 8)),
             dma((15,)), dma((15,)), dma((7,)), dma((7,)), dma((15,)), dma((15,)),
         ],

time: 84.4 us -> 79.5 us (0.942)
  Pallas kernels: 83.6 us -> 78.7 us
    pallas_call x1, Pallas kernels: 81.8 us -> 76.8 us  [body(): pl.pallas_call(functools.partial(step_kernel, channels, points * lax.axis...]
where the time goes in v4:
time: 79.5 us; the launch traced here: 79.3 us
  Pallas kernels  78.7 us (99%)
    pallas_call x1, Pallas kernels, body(): pl.pallas_call(functools.partial(step_kernel, channels, points * lax.axis...  76.8 us
    pallas_call x1, Pallas kernels, body(): pl.pallas_call(functools.partial(finish_kernel, channels), out_shape=(jax...  1.88 us

profile of v4, /device:TPU:6, one launch (start us, length us, event | category | flops | bytes accessed | tf_op | source)
XLA Modules:
  0.0 79.3 jit_solution(2460756781620514963)
XLA Ops:
  0.6 76.8 %step.1 = (f32[4,32,128]{2,1,0:T(8,128)}, bf16[16,8,512]{2,1,0:T(8,128)(2,1)}, bf16[16,8,512]{2,1,0:T(8,128)(2,1)}) custom-call(bf16[128,1024]{1,0:T(8,128)(2,1)} %bitcast.3, bf16[128,1024]{1,0:T(8,128)(2,1)} %bitcast.4, s32[1,128]{1,0:T(1,128)} %index_ref.1, f32[100,128]{1,0:T(8,128)} %target_ref.1, bf16[1024,1024]{1,0:T(8,128)(2,1)} %wq_ref.1, ...), custom_call_target="tpu_custom_call" | custom-call | tf_op jit(solution)/shard_map/step/pallas_call | solution.py:520
  77.4 1.9 %finish.1 = (f32[1,1]{1,0:T(1,128)}, f32[100,1024]{1,0:T(8,128)}, f32[64,64]{1,0:T(8,128)}, f32[64,64]{1,0:T(8,128)}, f32[64,64]{1,0:T(8,128)}, /*index=5*/f32[64,64]{1,0:T(8,128)}) custom-call(f32[4,32,128]{2,1,0:T(8,128)} %get-tuple-element.15.grads_ref, bf16[16,8,512]{2,1,0:T(8,128)(2,1)} %get-tuple-element.16.g3, bf16[16,8,512]{2,1,0:T(8,128)(2,1)} %get-tuple-element.17.g4), custom_call_target="tpu_custom_call" | custom-call | tf_op jit(solution)/shard_map/finish/pallas_call | solution.py:570

commit v5 on v4

--- a/solution.py
+++ b/solution.py
@@ -120,7 +120,7 @@
             dst[128 * n : 128 * n + 128, :] = source[:, 128 * n : 128 * n + 128].T
 
     loads[0].wait()
-    turned(grids.at[y, core], acts_ref[1])
+    turned(grids.at[x, core], acts_ref[1])
     loads[2].wait()
     wide_dot(acts_ref[1], wq, queries)
     place = (index_ref[...] - (space - 1) * 128 + 2048) & 2047
@@ -143,7 +143,7 @@
     def on_y(p, c):
         return device(x, p, z, c)
 
-    tiles = ((nodes, x, on_x), (grids, y, on_y), (mixes, y, on_y))
+    tiles = ((nodes, y, on_y), (grids, x, on_x), (mixes, x, on_x))
     ring = {}
 
     def move(i, k, ref, target):
@@ -181,19 +181,20 @@
     ]
     pair = {}
     pair = {}
-    spread_tile(1)
     for copy in halo:
         copy.wait_recv()
     for n in range(4):
         cut = slice(256 * n, 256 * n + 256)
         found = sum(across(chosen[128 * i : 128 * i + 128], near[i, :, cut]) for i in range(3))
         acts_ref[0, :, cut] = found.astype(BF16)
+    spread_tile(1)
+    turned(nodes.at[y, core], acts_ref[0])
+    spread_tile(0)
     loads[3].wait()
     wide_dot(acts_ref[0], wk, keyset)
     loads[4].wait()
     wide_dot(acts_ref[0], wv, valueset)
 
-    forward_tile(1)
     early = lax.broadcasted_iota(jnp.int32, (128, 128), 1) < 64
 
     def apart_heads(v):
@@ -226,8 +227,9 @@
         send(field.at[t[0]], seen.at[ens], (ssem.at[d], rsem.at[d]), t) for d, t in enumerate(ens_others)
     ]
     seen[ens] = field[ens]
-    turned(nodes.at[x, core], acts_ref[0])
-    spread_tile(0)
+    turned(mixes.at[x, core], acts_ref[2])
+    spread_tile(2)
+    forward_tile(1)
     for copy in sends:
         copy.wait_recv()
     weight = (channels * points_all) ** (-0.5)
@@ -256,8 +258,7 @@
         send(out.at[t[0]], slopes.at[ens], (bsem.at[d], csem.at[d]), t) for d, t in enumerate(ens_others)
     ]
     slopes[ens] = out[ens]
-    turned(mixes.at[y, core], acts_ref[2])
-    spread_tile(2)
+    forward_tile(0)
     close_tile(1)
     total = weight * (skill * (1.0 / 16) - pair_weight * spread)
     channel = ens * 8 + lax.broadcasted_iota(jnp.int32, (8, 128), 0)
@@ -301,13 +302,20 @@
         right = d_hidden[:, 128 * n + 512 : 128 * n + 640].astype(F32)
         m_out[0, n], m_out[1, n] = by_parity(left, right)
     for k in (4, 5, 2, 3, 6, 7, 1):
-        exchange(2, k, m_out, m_in, (y, on_y))
-    m_in[y, core] = m_out[core, y]
+        exchange(2, k, m_out, m_in, (x, on_x))
+    m_in[x, core] = m_out[core, x]
+    readout_gradient()
+    pair["half"] = send(halves.at[1 - core], half_in, (pair_s.at[5], pair_r.at[5]), partner)
+
     for n in range(4):
         cut = slice(256 * n, 256 * n + 256)
         d_attended[:, cut] = columns(d_hidden[...], wm[cut, :]).astype(BF16)
 
-    forward_tile(0)
+    pair["half"].wait_recv()
+    half_sum[...] = (halves[core].astype(F32) + half_in[...].astype(F32)).astype(BF16)
+    gather1 = [
+        send(half_sum.at[t[0]], g1.at[d], (as1.at[d], ar1.at[d]), t) for d, t in enumerate(ens_others)
+    ]
     forward_tile(2)
     def join(v):
         return jnp.where(early, v[0:128], v[128:256])
@@ -330,81 +338,81 @@
         return d_keys, d_values, d_queries
 
     for d in (2, 1, 3, 0):
-        to = (x + d) % 4
+        to = (y + d) % 4
         kinds = list(zip(retreat(to), retreat(to + 4)))
         for i in range(2):
             kv_out[0, to, i], kv_out[1, to, i] = by_parity(*kinds[i])
         q_out[0, to], q_out[1, to] = by_parity(*kinds[2])
         for k in (2 * d, 2 * d + 1):
             if k:
-                exchange(0, k, kv_out, kv_in, (x, on_x))
+                exchange(0, k, kv_out, kv_in, (y, on_y))
     for k in (4, 5, 2, 3, 6, 7, 1):
-        exchange(1, k, q_out, q_in, (y, on_y))
-    kv_in[x, core] = kv_out[core, x]
-    q_in[y, core] = q_out[core, y]
+        exchange(1, k, q_out, q_in, (x, on_x))
+    kv_in[y, core] = kv_out[core, y]
+    q_in[x, core] = q_out[core, x]
     close_tile(0)
     close_tile(2)
-    readout_gradient()
-    pair["half"] = send(halves.at[1 - core], half_in, (pair_s.at[5], pair_r.at[5]), partner)
-
-    pair["half"].wait_recv()
-    half_sum[...] = (halves[core].astype(F32) + half_in[...].astype(F32)).astype(BF16)
-    gather1 = [
-        send(half_sum.at[t[0]], g1.at[d], (as1.at[d], ar1.at[d]), t) for d, t in enumerate(ens_others)
-    ]
-
-
-    def store(base, step, left, right):
+
+
+    def store(base, w, left, right):
         for h, block in enumerate(by_parity(left, right)):
-            for w in range(4):
+            for step in range(4):
                 for r in range(2):
-                    row = w * 64 + r * 32
+                    row = step * 64 + r * 32
                     work[base + r, w, h * 4 + step] = block[row : row + 32]
 
-    def product(buf, at, right):
+    def product(buf, w, right):
         total = None
         for t in range(4):
-            left = jnp.concatenate([buf[t, 0, at, :], buf[t, 1, at, :]], axis=1)
-            term = dot32(left, right(t))
+            sides = []
+            for c in range(2):
+                strips = [buf[t, c, pl.ds(pl.multiple_of(n * 256 + w * 64, 64), 64), :] for n in range(4)]
+                sides.append(jnp.concatenate(strips, axis=0))
+            term = dot32(jnp.concatenate(sides, axis=1), right(t))
             total = term if total is None else total + term
         return total
 
     def keys_values(t):
         return jnp.concatenate([kv_in[t, :, i].reshape(256, 128) for i in range(2)], axis=1)
 
-    def first_product(step, carry):
-        found = product(nodes, pl.ds(pl.multiple_of(step * 256, 256), 256), keys_values)
-        store(0, step, found[:, 0:128], found[:, 128:256])
+    def first_product(w):
+        found = product(nodes, w, keys_values)
+        store(0, w, found[:, 0:128], found[:, 128:256])
+
+    def mix_product(w, carry):
+        mixed[w] = product(mixes, w, lambda t: m_in[t].reshape(256, 128))
         return carry
 
-    def mix_product(step, carry):
-        at = pl.ds(pl.multiple_of(step * 256, 256), 256)
-        mixed[at, :] = product(mixes, at, lambda t: m_in[t].reshape(256, 128))
-        return carry
-
-    def second_product(step, carry):
-        at = pl.ds(pl.multiple_of(step * 256, 256), 256)
-        store(2, step, product(grids, at, lambda t: q_in[t].reshape(256, 128)), mixed[at, :])
-        return carry
+    def second_product(w):
+        store(2, w, product(grids, w, lambda t: q_in[t].reshape(256, 128)), mixed[w])
 
     flips = [(flip1, flip3), (flip3, flip1)] * 2
-    places = [(y, on_y), (y, on_y), (x, on_x), (x, on_x)]
+    places = [(x, on_x), (x, on_x), (y, on_y), (y, on_y)]
     third, fourth = {}, {}
 
-    def halve(c):
+    def halve(c, slot):
         f1, f2 = flips[c]
         q, beside = places[c]
-        for slot, block in ((1, f2(f1(q))), (0, f1(q))):
-            third[c, slot] = send(
-                work.at[c, block], r3.at[c, slot], (s3.at[c, slot], q3.at[c, slot]), beside(f1(q), core)
-            )
+        block = f2(f1(q)) if slot else f1(q)
+        third[c, slot] = send(
+            work.at[c, block], r3.at[c, slot], (s3.at[c, slot], q3.at[c, slot]), beside(f1(q), core)
+        )
+
+    def reduce_blocks(base, compute):
+        q = places[base][0]
+        compute(flip3(flip1(q)))
+        halve(base, 1)
+        halve(base + 1, 1)
+        compute(flip1(q))
+        halve(base, 0)
+        compute(flip3(q))
+        halve(base + 1, 0)
+        compute(q)
 
     for k in range(1, 8):
         parts[0, k].wait_recv()
     have_tile(0)
-    lax.fori_loop(0, 4, first_product, 0)
-    halve(0)
-    halve(1)
+    reduce_blocks(0, first_product)
     for k in range(1, 8):
         parts[2, k].wait_recv()
     have_tile(2)
@@ -421,9 +429,7 @@
     for k in range(1, 8):
         parts[1, k].wait_recv()
     have_tile(1)
-    lax.fori_loop(0, 4, second_product, 0)
-    halve(2)
-    halve(3)
+    reduce_blocks(2, second_product)
 
     for c in range(4):
         f1, f2 = flips[c]
@@ -431,6 +437,32 @@
         third[c, 1].wait_recv()
         work[c, f2(q)] = (work[c, f2(q)].astype(F32) + r3[c, 1].astype(F32)).astype(BF16)
         fourth[c] = send(work.at[c, f2(q)], r4.at[c], (s4.at[c], q4.at[c]), beside(f2(q), core))
+    deep = []
+
+    def settle(i):
+        for c in (2 * i, 2 * i + 1):
+            q = places[c][0]
+            third[c, 0].wait_recv()
+            fourth[c].wait_recv()
+            block = work[c, q].astype(F32) + r3[c, 0].astype(F32) + r4[c].astype(F32)
+            block = block.astype(BF16)
+            for k in range(8):
+                last[i, k, c % 2] = block[k]
+        for d in (4, 3, 5, 2, 6, 1, 7):
+            target = mirrored[d] if i == 0 else z_others[d - 1]
+            deep.append(send(last.at[i, (z + d) % 8], rz.at[i, d], (zs.at[i, d], zr.at[i, d]), target))
+
+    settle(0)
+    mirror = remote(last.at[0, z], rz.at[0, 0], (zs.at[0, 0], zr.at[0, 0]), mirrored[0])
+
+    @pl.when(x != y)
+    def _():
+        mirror.start()
+
+    @pl.when(x == y)
+    def _():
+        rz[0, 0] = last[0, z]
+
     for copy in gather2:
         copy.wait_recv()
     summed = own2[...].astype(F32)
@@ -442,29 +474,7 @@
     ]
     g3[ens] = own3[...]
 
-    deep = []
-    for i in range(2):
-        for c in (2 * i, 2 * i + 1):
-            q = places[c][0]
-            third[c, 0].wait_recv()
-            fourth[c].wait_recv()
-            block = work[c, q].astype(F32) + r3[c, 0].astype(F32) + r4[c].astype(F32)
-            block = block.astype(BF16)
-            for k in range(8):
-                last[i, k, c % 2] = block[k]
-        for d in range(1, 8):
-            target = z_others[d - 1] if i == 0 else mirrored[d]
-            deep.append(send(last.at[i, (z + d) % 8], rz.at[i, d], (zs.at[i, d], zr.at[i, d]), target))
-    mirror = remote(last.at[1, z], rz.at[1, 0], (zs.at[1, 0], zr.at[1, 0]), mirrored[0])
-
-    @pl.when(x != y)
-    def _():
-        mirror.start()
-
-    @pl.when(x == y)
-    def _():
-        rz[1, 0] = last[1, z]
-
+    settle(1)
     for copy in gather3:
         copy.wait_recv()
     final = send(g3, g4, (pair_s.at[6], pair_r.at[6]), partner)
@@ -476,7 +486,7 @@
         mirror.wait()
 
     for i in range(2):
-        grads = (last[0, z] if i == 0 else rz[1, 0]).astype(F32)
+        grads = (rz[0, 0] if i == 0 else last[1, z]).astype(F32)
         for d in range(1, 8):
             grads = grads + rz[i, d].astype(F32)
         grads_ref[2 * i : 2 * i + 2] = grads
@@ -537,7 +547,7 @@
             vmem(4, 2, 2, 128, 128),
             vmem(4, 2, 128, 128),
             vmem(4, 2, 128, 128),
-            pltpu.VMEM((1024, 128), F32),
+            pltpu.VMEM((4, 256, 128), F32),
             vmem(4, 2, 1024, 128),
             vmem(4, 2, 1024, 128),
             vmem(4, 2, 1024, 128),

time: 79.5 us -> 80.9 us (1.018)
  the two profiles are of different devices: /device:TPU:6 before, /device:TPU:8 now
where the time goes in v5:
time: 80.9 us; the launch traced here: 80.8 us
  Pallas kernels  80.1 us (99%)
    pallas_call x1, Pallas kernels, body(): pl.pallas_call(functools.partial(step_kernel, channels, points * lax.axis...  78.3 us
    pallas_call x1, Pallas kernels, body(): pl.pallas_call(functools.partial(finish_kernel, channels), out_shape=(jax...  1.88 us

profile of v5, /device:TPU:8, one launch (start us, length us, event | category | flops | bytes accessed | tf_op | source)
XLA Modules:
  0.0 80.8 jit_solution(5918544511936735015)
XLA Ops:
  0.6 78.3 %step.1 = (f32[4,32,128]{2,1,0:T(8,128)}, bf16[16,8,512]{2,1,0:T(8,128)(2,1)}, bf16[16,8,512]{2,1,0:T(8,128)(2,1)}) custom-call(bf16[128,1024]{1,0:T(8,128)(2,1)} %bitcast.3, bf16[128,1024]{1,0:T(8,128)(2,1)} %bitcast.4, s32[1,128]{1,0:T(1,128)} %index_ref.1, f32[100,128]{1,0:T(8,128)} %target_ref.1, bf16[1024,1024]{1,0:T(8,128)(2,1)} %wq_ref.1, ...), custom_call_target="tpu_custom_call" | custom-call | tf_op jit(solution)/shard_map/step/pallas_call | solution.py:530
  78.9 1.9 %finish.1 = (f32[1,1]{1,0:T(1,128)}, f32[100,1024]{1,0:T(8,128)}, f32[64,64]{1,0:T(8,128)}, f32[64,64]{1,0:T(8,128)}, f32[64,64]{1,0:T(8,128)}, /*index=5*/f32[64,64]{1,0:T(8,128)}) custom-call(f32[4,32,128]{2,1,0:T(8,128)} %get-tuple-element.15.grads_ref, bf16[16,8,512]{2,1,0:T(8,128)(2,1)} %get-tuple-element.16.g3, bf16[16,8,512]{2,1,0:T(8,128)(2,1)} %get-tuple-element.17.g4), custom_call_target="tpu_custom_call" | custom-call | tf_op jit(solution)/shard_map/finish/pallas_call | solution.py:580

commit v6 on v4

--- a/solution.py
+++ b/solution.py
@@ -188,21 +188,14 @@
         cut = slice(256 * n, 256 * n + 256)
         found = sum(across(chosen[128 * i : 128 * i + 128], near[i, :, cut]) for i in range(3))
         acts_ref[0, :, cut] = found.astype(BF16)
-    loads[3].wait()
-    wide_dot(acts_ref[0], wk, keyset)
-    loads[4].wait()
-    wide_dot(acts_ref[0], wv, valueset)
-
-    forward_tile(1)
     early = lax.broadcasted_iota(jnp.int32, (128, 128), 1) < 64
 
     def apart_heads(v):
         zero = jnp.zeros_like(v)
         return jnp.concatenate([jnp.where(early, v, zero), jnp.where(early, zero, v)], axis=0)
 
-    def attend(h, carry):
-        at = pl.ds(pl.multiple_of(h * 128, 128), 128)
-        scores = columns(queries[:, at], apart_heads(keyset[:, at])) * 0.125
+    def attend(h, keys, values):
+        scores = columns(queries[:, 128 * h : 128 * h + 128], apart_heads(keys)) * 0.125
         halves_of = []
         for i in range(2):
             part = scores[:, 128 * i : 128 * i + 128]
@@ -210,13 +203,22 @@
             halves_of.append(raised / jnp.sum(raised, axis=-1, keepdims=True))
         soft = jnp.concatenate(halves_of, axis=1)
         probs[h] = soft
-        acts_ref[2, :, at] = dot32(soft.astype(BF16), apart_heads(valueset[:, at])).astype(BF16)
-        return carry
-
-    lax.fori_loop(0, 8, attend, 0, unroll=2)
+        acts_ref[2, :, 128 * h : 128 * h + 128] = dot32(soft.astype(BF16), apart_heads(values)).astype(BF16)
+
+    loads[3].wait()
+    loads[4].wait()
+    for n in range(4):
+        cut = slice(256 * n, 256 * n + 256)
+        keys = dot32(acts_ref[0], wk[:, cut]).astype(BF16)
+        values = dot32(acts_ref[0], wv[:, cut]).astype(BF16)
+        keyset[:, cut] = keys
+        valueset[:, cut] = values
+        for i in range(2):
+            side = slice(128 * i, 128 * i + 128)
+            attend(2 * n + i, keys[:, side], values[:, side])
+    forward_tile(1)
     loads[5].wait()
-    wide_dot(acts_ref[2], wm, hidden)
-    full = hidden[...] + acts_ref[1].astype(F32)
+    full = dot32(acts_ref[2], wm[...]) + acts_ref[1].astype(F32)
     inverse = lax.rsqrt(jnp.sum(full * full, axis=-1, keepdims=True) * (1.0 / 1024) + EPS)
     hidden[...] = full * inverse
     normed_b = hidden[...].astype(BF16)
@@ -303,10 +305,18 @@
     for k in (4, 5, 2, 3, 6, 7, 1):
         exchange(2, k, m_out, m_in, (y, on_y))
     m_in[y, core] = m_out[core, y]
+    readout_gradient()
+    pair["half"] = send(halves.at[1 - core], half_in, (pair_s.at[5], pair_r.at[5]), partner)
+
     for n in range(4):
         cut = slice(256 * n, 256 * n + 256)
         d_attended[:, cut] = columns(d_hidden[...], wm[cut, :]).astype(BF16)
 
+    pair["half"].wait_recv()
+    half_sum[...] = (halves[core].astype(F32) + half_in[...].astype(F32)).astype(BF16)
+    gather1 = [
+        send(half_sum.at[t[0]], g1.at[d], (as1.at[d], ar1.at[d]), t) for d, t in enumerate(ens_others)
+    ]
     forward_tile(0)
     forward_tile(2)
     def join(v):
@@ -344,14 +354,6 @@
     q_in[y, core] = q_out[core, y]
     close_tile(0)
     close_tile(2)
-    readout_gradient()
-    pair["half"] = send(halves.at[1 - core], half_in, (pair_s.at[5], pair_r.at[5]), partner)
-
-    pair["half"].wait_recv()
-    half_sum[...] = (halves[core].astype(F32) + half_in[...].astype(F32)).astype(BF16)
-    gather1 = [
-        send(half_sum.at[t[0]], g1.at[d], (as1.at[d], ar1.at[d]), t) for d, t in enumerate(ens_others)
-    ]
 
 
     def store(base, step, left, right):
@@ -431,6 +433,22 @@
         third[c, 1].wait_recv()
         work[c, f2(q)] = (work[c, f2(q)].astype(F32) + r3[c, 1].astype(F32)).astype(BF16)
         fourth[c] = send(work.at[c, f2(q)], r4.at[c], (s4.at[c], q4.at[c]), beside(f2(q), core))
+    deep = []
+
+    def settle(i):
+        for c in (2 * i, 2 * i + 1):
+            q = places[c][0]
+            third[c, 0].wait_recv()
+            fourth[c].wait_recv()
+            block = work[c, q].astype(F32) + r3[c, 0].astype(F32) + r4[c].astype(F32)
+            block = block.astype(BF16)
+            for k in range(8):
+                last[i, k, c % 2] = block[k]
+        for d in (4, 3, 5, 2, 6, 1, 7):
+            target = z_others[d - 1] if i == 0 else mirrored[d]
+            deep.append(send(last.at[i, (z + d) % 8], rz.at[i, d], (zs.at[i, d], zr.at[i, d]), target))
+
+    settle(0)
     for copy in gather2:
         copy.wait_recv()
     summed = own2[...].astype(F32)
@@ -442,19 +460,7 @@
     ]
     g3[ens] = own3[...]
 
-    deep = []
-    for i in range(2):
-        for c in (2 * i, 2 * i + 1):
-            q = places[c][0]
-            third[c, 0].wait_recv()
-            fourth[c].wait_recv()
-            block = work[c, q].astype(F32) + r3[c, 0].astype(F32) + r4[c].astype(F32)
-            block = block.astype(BF16)
-            for k in range(8):
-                last[i, k, c % 2] = block[k]
-        for d in range(1, 8):
-            target = z_others[d - 1] if i == 0 else mirrored[d]
-            deep.append(send(last.at[i, (z + d) % 8], rz.at[i, d], (zs.at[i, d], zr.at[i, d]), target))
+    settle(1)
     mirror = remote(last.at[1, z], rz.at[1, 0], (zs.at[1, 0], zr.at[1, 0]), mirrored[0])
 
     @pl.when(x != y)
@@ -560,7 +566,7 @@
             dma((15,)), dma((15,)), dma((7,)), dma((7,)), dma((15,)), dma((15,)),
         ],
         compiler_params=pltpu.CompilerParams(
-            collective_id=1, has_side_effects=True, vmem_limit_bytes=56 << 20
+            collective_id=1, has_side_effects=True, vmem_limit_bytes=44 << 20
         ),
         name="step",
     )(
@@ -576,6 +582,7 @@
         ),
         in_specs=[whole] * 3,
         out_specs=(pl.BlockSpec(memory_space=pltpu.SMEM),) + (whole,) * 5,
+        compiler_params=pltpu.CompilerParams(vmem_limit_bytes=4 << 20),
         name="finish",
     )(grads, g3, g4)
     return loss.reshape(()), grad_out, grad_query, grad_key, grad_value, grad_mix

time: 79.5 us -> 83.2 us (1.047); the launches traced: 79.3 us -> 81.7 us
  local copies, waits for them, and re-layouts: 0 us -> 10.6 us
  Pallas kernels: 78.7 us -> 70.4 us
    unnamed x0 -> x18, local copies, waits for them, and re-layouts: none -> 10.6 us
    pallas_call x1, Pallas kernels: 76.8 us -> 69.5 us  [body(): pl.pallas_call(functools.partial(step_kernel, channels, points * lax.axis...]
    pallas_call x1, Pallas kernels: 1.88 us -> 0.88 us  [body(): pl.pallas_call(functools.partial(finish_kernel, channels), out_shape=(jax...]
where the time goes in v6:
time: 83.2 us; the launch traced here: 81.7 us
  Pallas kernels  70.4 us (85%)
  local copies, waits for them, and re-layouts  10.6 us (13%)
    pallas_call x1, Pallas kernels, body(): pl.pallas_call(functools.partial(step_kernel, channels, points * lax.axis...  69.5 us
    unnamed x18, local copies, waits for them, and re-layouts  10.6 us

profile of v6, /device:TPU:6, one launch (start us, length us, event | category | flops | bytes accessed | tf_op | source)
XLA Modules:
  0.0 81.7 jit_solution(7373699396322038023)
XLA Ops:
  0.6 0.0 copy-start
  0.6 1.6 %copy-done = bf16[1024,1024]{1,0:T(8,128)(2,1)S(1)} copy-done((bf16[1024,1024]{1,0:T(8,128)(2,1)S(1)}, bf16[1024,1024]{1,0:T(8,128)(2,1)}, u32[]{:S(2)}) %copy-start) | copy-done | bytes 2097176
  2.2 0.0 copy-start.1
  2.2 1.6 %copy-done.1 = bf16[1024,1024]{1,0:T(8,128)(2,1)S(1)} copy-done((bf16[1024,1024]{1,0:T(8,128)(2,1)S(1)}, bf16[1024,1024]{1,0:T(8,128)(2,1)}, u32[]{:S(2)}) %copy-start.1) | copy-done | bytes 2097176
  3.8 0.0 copy-start.2
  3.8 1.6 %copy-done.2 = bf16[1024,1024]{1,0:T(8,128)(2,1)S(1)} copy-done((bf16[1024,1024]{1,0:T(8,128)(2,1)S(1)}, bf16[1024,1024]{1,0:T(8,128)(2,1)}, u32[]{:S(2)}) %copy-start.2) | copy-done | bytes 2097176
  5.4 0.0 copy-start.3
  5.4 1.6 %copy-done.3 = bf16[1024,1024]{1,0:T(8,128)(2,1)S(1)} copy-done((bf16[1024,1024]{1,0:T(8,128)(2,1)S(1)}, bf16[1024,1024]{1,0:T(8,128)(2,1)}, u32[]{:S(2)}) %copy-start.3) | copy-done | bytes 2097176
  7.0 0.0 copy-start.4
  7.0 0.9 %copy-done.4 = bf16[1,128,1024]{2,1,0:T(8,128)(2,1)S(1)} copy-done((bf16[1,128,1024]{2,1,0:T(8,128)(2,1)S(1)}, bf16[1,128,1024]{2,1,0:T(8,128)(2,1)}, u32[]{:S(2)}) %copy-start.4) | copy-done | bytes 262168
  8.0 0.0 copy-start.5
  8.0 0.9 %copy-done.5 = bf16[1,128,1024]{2,1,0:T(8,128)(2,1)S(1)} copy-done((bf16[1,128,1024]{2,1,0:T(8,128)(2,1)S(1)}, bf16[1,128,1024]{2,1,0:T(8,128)(2,1)}, u32[]{:S(2)}) %copy-start.5) | copy-done | bytes 262168
  8.9 0.0 copy-start.6
  8.9 0.9 %copy-done.6 = bf16[100,1024]{1,0:T(8,128)(2,1)S(1)} copy-done((bf16[100,1024]{1,0:T(8,128)(2,1)S(1)}, bf16[100,1024]{1,0:T(8,128)(2,1)}, u32[]{:S(2)}) %copy-start.6) | copy-done | bytes 204824
  9.8 0.0 copy-start.7
  9.8 0.8 copy-done.7
  10.6 0.0 copy-start.8
  10.6 0.7 copy-done.8
  11.3 69.5 %step.1 = (f32[4,32,128]{2,1,0:T(8,128)S(1)}, bf16[16,8,512]{2,1,0:T(8,128)(2,1)S(1)}, bf16[16,8,512]{2,1,0:T(8,128)(2,1)S(1)}) custom-call(bf16[128,1024]{1,0:T(8,128)(2,1)S(1)} %bitcast.3, bf16[128,1024]{1,0:T(8,128)(2,1)S(1)} %bitcast.4, s32[1,128]{1,0:T(1,128)S(1)} %copy-done.8, f32[100,128]{1,0:T(8,128)S(1)} %copy-done.7, ...), custom_call_target="tpu_custom_call" | custom-call | tf_op jit(solution)/shard_map/step/pallas_call | solution.py:526
  80.8 0.9 %finish.1 = (f32[1,1]{1,0:T(1,128)}, f32[100,1024]{1,0:T(8,128)}, f32[64,64]{1,0:T(8,128)}, f32[64,64]{1,0:T(8,128)}, f32[64,64]{1,0:T(8,128)}, /*index=5*/f32[64,64]{1,0:T(8,128)}) custom-call(f32[4,32,128]{2,1,0:T(8,128)S(1)} %get-tuple-element.15.grads_ref, bf16[16,8,512]{2,1,0:T(8,128)(2,1)S(1)} %get-tuple-element.16.g3, ...), custom_call_target="tpu_custom_call" | custom-call | tf_op jit(solution)/shard_map/finish/pallas_call | solution.py:576
Async XLA Ops:
  0.6 1.6 %copy-start = (bf16[1024,1024]{1,0:T(8,128)(2,1)S(1)}, bf16[1024,1024]{1,0:T(8,128)(2,1)}, u32[]{:S(2)}) copy-start(bf16[1024,1024]{1,0:T(8,128)(2,1)} %wq_ref.1) | copy-start | bytes 6291460
  2.2 1.6 %copy-start.1 = (bf16[1024,1024]{1,0:T(8,128)(2,1)S(1)}, bf16[1024,1024]{1,0:T(8,128)(2,1)}, u32[]{:S(2)}) copy-start(bf16[1024,1024]{1,0:T(8,128)(2,1)} %wk_ref.1) | copy-start | bytes 6291460
  3.8 1.6 %copy-start.2 = (bf16[1024,1024]{1,0:T(8,128)(2,1)S(1)}, bf16[1024,1024]{1,0:T(8,128)(2,1)}, u32[]{:S(2)}) copy-start(bf16[1024,1024]{1,0:T(8,128)(2,1)} %wv_ref.1) | copy-start | bytes 6291460
  5.4 1.6 %copy-start.3 = (bf16[1024,1024]{1,0:T(8,128)(2,1)S(1)}, bf16[1024,1024]{1,0:T(8,128)(2,1)}, u32[]{:S(2)}) copy-start(bf16[1024,1024]{1,0:T(8,128)(2,1)} %wm_ref.1) | copy-start | bytes 6291460
  7.0 0.9 %copy-start.4 = (bf16[1,128,1024]{2,1,0:T(8,128)(2,1)S(1)}, bf16[1,128,1024]{2,1,0:T(8,128)(2,1)}, u32[]{:S(2)}) copy-start(bf16[1,128,1024]{2,1,0:T(8,128)(2,1)} %param.9) | copy-start | bytes 786436
  8.0 0.9 %copy-start.5 = (bf16[1,128,1024]{2,1,0:T(8,128)(2,1)S(1)}, bf16[1,128,1024]{2,1,0:T(8,128)(2,1)}, u32[]{:S(2)}) copy-start(bf16[1,128,1024]{2,1,0:T(8,128)(2,1)} %param.10) | copy-start | bytes 786436
  8.9 0.9 %copy-start.6 = (bf16[100,1024]{1,0:T(8,128)(2,1)S(1)}, bf16[100,1024]{1,0:T(8,128)(2,1)}, u32[]{:S(2)}) copy-start(bf16[100,1024]{1,0:T(8,128)(2,1)} %readout_ref.1) | copy-start | bytes 614404
  9.8 0.8 copy-start.7
  10.6 0.7 copy-start.8

commit v7 on v6

--- a/solution.py
+++ b/solution.py
@@ -566,7 +566,7 @@
             dma((15,)), dma((15,)), dma((7,)), dma((7,)), dma((15,)), dma((15,)),
         ],
         compiler_params=pltpu.CompilerParams(
-            collective_id=1, has_side_effects=True, vmem_limit_bytes=44 << 20
+            collective_id=1, has_side_effects=True, vmem_limit_bytes=56 << 20
         ),
         name="step",
     )(
@@ -582,7 +582,6 @@
         ),
         in_specs=[whole] * 3,
         out_specs=(pl.BlockSpec(memory_space=pltpu.SMEM),) + (whole,) * 5,
-        compiler_params=pltpu.CompilerParams(vmem_limit_bytes=4 << 20),
         name="finish",
     )(grads, g3, g4)
     return loss.reshape(()), grad_out, grad_query, grad_key, grad_value, grad_mix

time: 83.2 us -> 75.2 us (0.904)
  local copies, waits for them, and re-layouts: 10.6 us -> 0 us
  Pallas kernels: 70.4 us -> 73.6 us
    unnamed x18 -> x0, local copies, waits for them, and re-layouts: 10.6 us -> none
    pallas_call x1, Pallas kernels: 69.5 us -> 71.7 us  [body(): pl.pallas_call(functools.partial(step_kernel, channels, points * lax.axis...]
    pallas_call x1, Pallas kernels: 0.88 us -> 1.88 us  [body(): pl.pallas_call(functools.partial(finish_kernel, channels), out_shape=(jax...]
where the time goes in v7:
time: 75.2 us; the launch traced here: 74.2 us
  Pallas kernels  73.6 us (98%)
    pallas_call x1, Pallas kernels, body(): pl.pallas_call(functools.partial(step_kernel, channels, points * lax.axis...  71.7 us
    pallas_call x1, Pallas kernels, body(): pl.pallas_call(functools.partial(finish_kernel, channels), out_shape=(jax...  1.88 us

profile of v7, /device:TPU:6, one launch (start us, length us, event | category | flops | bytes accessed | tf_op | source)
XLA Modules:
  0.0 74.2 jit_solution(2732996264908963800)
XLA Ops:
  0.6 71.7 %step.1 = (f32[4,32,128]{2,1,0:T(8,128)}, bf16[16,8,512]{2,1,0:T(8,128)(2,1)}, bf16[16,8,512]{2,1,0:T(8,128)(2,1)}) custom-call(bf16[128,1024]{1,0:T(8,128)(2,1)} %bitcast.3, bf16[128,1024]{1,0:T(8,128)(2,1)} %bitcast.4, s32[1,128]{1,0:T(1,128)} %index_ref.1, f32[100,128]{1,0:T(8,128)} %target_ref.1, bf16[1024,1024]{1,0:T(8,128)(2,1)} %wq_ref.1, ...), custom_call_target="tpu_custom_call" | custom-call | tf_op jit(solution)/shard_map/step/pallas_call | solution.py:526
  72.3 1.9 %finish.1 = (f32[1,1]{1,0:T(1,128)}, f32[100,1024]{1,0:T(8,128)}, f32[64,64]{1,0:T(8,128)}, f32[64,64]{1,0:T(8,128)}, f32[64,64]{1,0:T(8,128)}, /*index=5*/f32[64,64]{1,0:T(8,128)}) custom-call(f32[4,32,128]{2,1,0:T(8,128)} %get-tuple-element.15.grads_ref, bf16[16,8,512]{2,1,0:T(8,128)(2,1)} %get-tuple-element.16.g3, bf16[16,8,512]{2,1,0:T(8,128)(2,1)} %get-tuple-element.17.g4), custom_call_target="tpu_custom_call" | custom-call | tf_op jit(solution)/shard_map/finish/pallas_call | solution.py:576
